TPU v7x, 8 devices: a whole 2x2x1 slice. The times are simulated.
8 devices in a mesh: dp: 1 (over z), tp: 2 (over y), sp: 4 (over x, core).
Axes of the slice: x: 2, y: 2, z: 1, core: 2. Of those that a mesh axis runs over, the one named last changes fastest.
Arguments:
- k_cache: bfloat16 [4, 4, 4, 8192, 64], P(None, 'dp', 'tp', 'sp')
- v_cache: bfloat16 [4, 4, 4, 8192, 64], P(None, 'dp', 'tp', 'sp')
- lengths: int32 [4], P('dp')
- hidden: bfloat16 [4, 2048], P(('dp', 'sp'))
- ln_gain: bfloat16 [4, 2048], replicated
- w_query: bfloat16 [4, 2048, 2048], P(None, None, 'tp')
- w_key: bfloat16 [4, 2048, 256], P(None, None, 'tp')
- w_value: bfloat16 [4, 2048, 256], P(None, None, 'tp')
- w_out: bfloat16 [4, 2048, 2048], P(None, 'tp')
- w_gate: bfloat16 [4, 2048, 5632], P(None, None, 'tp')
- w_up: bfloat16 [4, 2048, 5632], P(None, None, 'tp')
- w_down: bfloat16 [4, 5632, 2048], P(None, 'tp')
Outputs:
- output 1: bfloat16 [4, 2048], P(('dp', 'sp'))
- output 2: bfloat16 [3, 4, 4, 4096, 64], P(None, ('dp', 'sp'), 'tp')
- output 3: bfloat16 [3, 4, 4, 4096, 64], P(None, ('dp', 'sp'), 'tp')
- output 4: bfloat16 [4, 4, 8192, 64], P(('dp', 'sp'), 'tp')
- output 5: bfloat16 [4, 4, 8192, 64], P(('dp', 'sp'), 'tp')
All inputs are finite; a program needn't handle non-finite values.
Results may differ from a plain program's by a relative error of at most 0.02.
Values are sent between devices in bfloat16 or wider.
A program may use at most 1 GiB of HBM per device.

v0:
```python
import functools

import jax
import jax.numpy as jnp
from jax import lax
from jax.experimental import pallas as pl
from jax.experimental.pallas import tpu as pltpu
from jax.sharding import PartitionSpec as P


WINDOW = 4096
ROPE_BASE = 50000
NORM_EPS = 1e-5
SHARD = 2048
CHUNK = 128
HEAD_DIM = 64
DEPTH = 4
TILE = 256
CROSS = [(0, 2), (2, 0), (1, 3), (3, 1)]
CROSS_SWAP = [(0, 3), (3, 0), (1, 2), (2, 1)]
PARTNER = [(0, 1), (1, 0), (2, 3), (3, 2)]


VMEM = pl.BlockSpec(memory_space=pltpu.VMEM)
SMEM = pl.BlockSpec(memory_space=pltpu.SMEM)
ANY = pl.BlockSpec(memory_space=pltpu.HBM)


def params(mib=40, **extra):
    return pltpu.CompilerParams(vmem_limit_bytes=mib * 2**20, **extra)


def place():
    sp = lax.axis_index("sp")
    return sp, lax.rem(sp, 2), sp // 2


def far_chunks(length, on_first_chip):
    turn = length - WINDOW
    start = jnp.where(on_first_chip, 0, (turn + 1) // CHUNK)
    count = jnp.where(on_first_chip, (turn + CHUNK - 1) // CHUNK, WINDOW // CHUNK - (turn + 1) // CHUNK)
    return start, count


def swap_kernel(layers, k_ref, v_ref, far_o, near_o, send_sem, recv_sem):
    sp, core, chip = place()
    peer = sp + 1 - 2 * core
    barrier = pltpu.get_barrier_semaphore()
    pl.semaphore_signal(barrier, inc=1, device_id={"sp": peer}, device_id_type=pl.DeviceIdType.MESH)
    pl.semaphore_wait(barrier, 1)
    far_rows = pl.ds(2 * (1 - chip), 2)

    def send(src, dst, i):
        return pltpu.make_async_remote_copy(
            src_ref=src, dst_ref=dst, send_sem=send_sem.at[i], recv_sem=recv_sem.at[i],
            device_id={"sp": peer}, device_id_type=pl.DeviceIdType.MESH)

    copies = []
    for i, (layer, sliding) in enumerate(layers):
        if sliding:
            @pl.when(core == 0)
            def _(layer=layer, i=i):
                send(v_ref.at[layer, far_rows], far_o.at[i], 3 * i).start()

            @pl.when(core == 1)
            def _(layer=layer, i=i):
                send(k_ref.at[layer, far_rows], far_o.at[i], 3 * i).start()

            copies.append(send(k_ref.at[layer, far_rows], far_o.at[i], 3 * i))
        pair = [send(k_ref.at[layer, peer], near_o.at[i, 0], 3 * i + 1),
                send(v_ref.at[layer, peer], near_o.at[i, 1], 3 * i + 2)]
        for copy in pair:
            copy.start()
        copies += pair
    for copy in copies:
        copy.wait()


def swap(layers, k_t, v_t, collective_id):
    n = len(layers)
    block = jax.ShapeDtypeStruct((n, 2, 2, HEAD_DIM, SHARD), jnp.bfloat16)
    return pl.pallas_call(
        functools.partial(swap_kernel, layers),
        out_shape=[block, block],
        in_specs=[ANY, ANY], out_specs=[ANY, ANY],
        scratch_shapes=[pltpu.SemaphoreType.DMA((3 * n,)), pltpu.SemaphoreType.DMA((3 * n,))],
        compiler_params=params(60, collective_id=collective_id, has_side_effects=True),
        cost_estimate=pl.CostEstimate(flops=10**9, bytes_accessed=4 * 2**20, transcendentals=0),
        name="swap",
    )(k_t, v_t)


def payload_kernel(layer, picks, k_ref, v_ref, *refs):
    sp, core, chip = place()
    rows = {"same": sp + 2 - 4 * chip, "cross": 2 * (1 - chip) + 1 - core}
    sems = refs[-1]
    copies = [pltpu.make_async_copy((k_ref, v_ref)[which].at[layer, rows[kind]], out, sems.at[i])
              for i, ((kind, which), out) in enumerate(zip(picks, refs))]
    for copy in copies:
        copy.start()
    for copy in copies:
        copy.wait()


def payload(layer, picks, k_t, v_t):
    block = jax.ShapeDtypeStruct((2, HEAD_DIM, SHARD), jnp.bfloat16)
    return pl.pallas_call(
        functools.partial(payload_kernel, layer, picks),
        out_shape=[block] * len(picks),
        in_specs=[ANY, ANY], out_specs=[VMEM] * len(picks),
        scratch_shapes=[pltpu.SemaphoreType.DMA((len(picks),))],
        compiler_params=params(60),
        cost_estimate=pl.CostEstimate(flops=10**9, bytes_accessed=len(picks) * 2**20, transcendentals=0),
        name="payload",
    )(k_t, v_t)


def swap_partials(part_ref, other_ref, sems):
    tp_peer = 1 - lax.axis_index("tp")
    barrier = pltpu.get_barrier_semaphore()
    pl.semaphore_signal(barrier, inc=1, device_id={"tp": tp_peer}, device_id_type=pl.DeviceIdType.MESH)
    pl.semaphore_wait(barrier, 1)
    copy = pltpu.make_async_remote_copy(
        src_ref=part_ref, dst_ref=other_ref, send_sem=sems.at[0], recv_sem=sems.at[1],
        device_id={"tp": tp_peer}, device_id_type=pl.DeviceIdType.MESH)
    copy.start()
    copy.wait()


def front_kernel(layer, sliding, exchange, *refs):
    if exchange:
        (h_ref, part_ref, gain_ref, cos_ref, sin_ref, wq, wk, wv, wg, wu, wd,
         q_o, k_o, v_o, m_o, h_o,
         wq_b, wk_b, wv_b, wg_b, wu_b, wd_b, qkv_sem, mlp_sem, other_ref, rdma_sem) = refs
    else:
        (h_ref, gain_ref, cos_ref, sin_ref, wq, wk, wv, wg, wu, wd,
         q_o, k_o, v_o, m_o, h_o,
         wq_b, wk_b, wv_b, wg_b, wu_b, wd_b, qkv_sem, mlp_sem) = refs
    n_tiles = wg.shape[2] // TILE
    qkv = [pltpu.make_async_copy(src.at[layer], dst, qkv_sem.at[i])
           for i, (src, dst) in enumerate(((wq, wq_b), (wk, wk_b), (wv, wv_b)))]

    def tile_copies(j, slot):
        cols = pl.ds(pl.multiple_of(j * TILE, TILE), TILE)
        return [pltpu.make_async_copy(wg.at[layer, :, cols], wg_b.at[slot], mlp_sem.at[0, slot]),
                pltpu.make_async_copy(wu.at[layer, :, cols], wu_b.at[slot], mlp_sem.at[1, slot]),
                pltpu.make_async_copy(wd.at[layer, cols, :], wd_b.at[slot], mlp_sem.at[2, slot])]

    for copy in qkv:
        copy.start()
    for j in range(DEPTH):
        for copy in tile_copies(j, j):
            copy.start()

    rows = h_ref[...].astype(jnp.float32)
    if exchange:
        swap_partials(part_ref, other_ref, rdma_sem)
        rows = (rows + (part_ref[...] + other_ref[...])).astype(jnp.bfloat16).astype(jnp.float32)
    h_o[...] = rows.astype(jnp.bfloat16)
    centered = rows - rows.mean(axis=-1, keepdims=True)
    variance = (centered * centered).mean(axis=-1, keepdims=True)
    scaled = centered * lax.rsqrt(variance + NORM_EPS)
    normed = (scaled * gain_ref[layer:layer + 1, :].astype(jnp.float32)).astype(jnp.bfloat16)
    normed = jnp.broadcast_to(normed, (8, normed.shape[1]))

    def rotate(x):
        if not sliding:
            return x
        width = x.shape[1]
        first = lax.broadcasted_iota(jnp.int32, x.shape, 1) % HEAD_DIM < HEAD_DIM // 2
        swapped = jnp.where(first, pltpu.roll(x, width - HEAD_DIM // 2, 1), pltpu.roll(x, HEAD_DIM // 2, 1))
        return x * cos_ref[:, :width] + swapped * sin_ref[:, :width]

    def query_step(j, carry):
        cols = pl.ds(pl.multiple_of(j * TILE, TILE), TILE)
        query = jnp.dot(normed, wq_b[:, cols], preferred_element_type=jnp.float32)
        q_o[:, cols] = rotate(query)[:1].astype(jnp.bfloat16)
        return carry

    for copy in qkv:
        copy.wait()
    lax.fori_loop(0, wq_b.shape[1] // TILE, query_step, 0)
    k_o[...] = rotate(jnp.dot(normed, wk_b[...], preferred_element_type=jnp.float32))[:1].astype(jnp.bfloat16)
    v_o[...] = jnp.dot(normed, wv_b[...], preferred_element_type=jnp.float32)[:1].astype(jnp.bfloat16)

    def tile_step(j, total):
        slot = lax.rem(j, DEPTH)
        for copy in tile_copies(j, slot):
            copy.wait()
        gate = jnp.dot(normed, wg_b[slot], preferred_element_type=jnp.float32)
        up = jnp.dot(normed, wu_b[slot], preferred_element_type=jnp.float32)
        act = (jax.nn.silu(gate) * up).astype(jnp.bfloat16)
        total = total + jnp.dot(act, wd_b[slot], preferred_element_type=jnp.float32)

        @pl.when(j + DEPTH < n_tiles)
        def _():
            for copy in tile_copies(j + DEPTH, slot):
                copy.start()

        return total

    total = lax.fori_loop(0, n_tiles, tile_step, jnp.zeros((8, m_o.shape[1]), jnp.float32))
    m_o[...] = total[:1]


def front(layer, sliding, h, part, gain, cos, sin, weights):
    exchange = part is not None
    dim = h.shape[1]
    q_width, kv_width = weights[0].shape[2], weights[1].shape[2]
    out = [jax.ShapeDtypeStruct((1, q_width), jnp.bfloat16), jax.ShapeDtypeStruct((1, kv_width), jnp.bfloat16),
           jax.ShapeDtypeStruct((1, kv_width), jnp.bfloat16), jax.ShapeDtypeStruct((1, dim), jnp.float32),
           jax.ShapeDtypeStruct((1, dim), jnp.bfloat16)]
    scratch = [pltpu.VMEM((dim, q_width), jnp.bfloat16), pltpu.VMEM((dim, kv_width), jnp.bfloat16),
               pltpu.VMEM((dim, kv_width), jnp.bfloat16), pltpu.VMEM((DEPTH, dim, TILE), jnp.bfloat16),
               pltpu.VMEM((DEPTH, dim, TILE), jnp.bfloat16), pltpu.VMEM((DEPTH, TILE, dim), jnp.bfloat16),
               pltpu.SemaphoreType.DMA((3,)), pltpu.SemaphoreType.DMA((3, DEPTH))]
    args = [h]
    extra = {}
    if exchange:
        args.append(part)
        scratch += [pltpu.VMEM((1, dim), jnp.float32), pltpu.SemaphoreType.DMA((2,))]
        extra = dict(collective_id=layer, has_side_effects=True)
    args += [gain, cos, sin]
    return pl.pallas_call(
        functools.partial(front_kernel, layer, sliding, exchange),
        out_shape=out,
        in_specs=[VMEM] * len(args) + [ANY] * 6,
        out_specs=[VMEM] * 5,
        scratch_shapes=scratch,
        compiler_params=params(**extra),
        cost_estimate=pl.CostEstimate(flops=6 * 10**9, bytes_accessed=40 * 10**6, transcendentals=0),
    )(*args, *weights)


def final_kernel(h_ref, part_ref, out_ref, other_ref, sems):
    swap_partials(part_ref, other_ref, sems)
    out_ref[...] = (h_ref[...].astype(jnp.float32) + (part_ref[...] + other_ref[...])).astype(jnp.bfloat16)


def final(h, part):
    return pl.pallas_call(
        final_kernel,
        out_shape=jax.ShapeDtypeStruct(h.shape, jnp.bfloat16),
        in_specs=[VMEM, VMEM], out_specs=VMEM,
        scratch_shapes=[pltpu.VMEM(part.shape, jnp.float32), pltpu.SemaphoreType.DMA((2,))],
        compiler_params=pltpu.CompilerParams(collective_id=8, has_side_effects=True),
        name="final",
    )(h, part)


def pack_kernel(layer, n_chunks, lengths, k_ref, v_ref, recv_ref, out_ref, sem):
    _, core, chip = place()
    far_row = 2 * (1 - chip)
    start0, count0 = far_chunks(lengths[far_row], chip == 1)
    start1, _ = far_chunks(lengths[far_row + 1], chip == 1)
    per_shard = SHARD // CHUNK

    def step(j, carry):
        second = j >= count0
        row = jnp.where(second, 1, 0)
        piece = jnp.clip(jnp.where(second, start1 + j - count0, start0 + j), 0, 2 * per_shard - 1)
        own = (piece // per_shard) == core
        lanes = pl.ds(pl.multiple_of(lax.rem(piece, per_shard) * CHUNK, CHUNK), CHUNK)

        @pl.when(own & (core == 0))
        def _():
            pltpu.make_async_copy(k_ref.at[layer, far_row + row, :, :, lanes], out_ref.at[j], sem).start()

        @pl.when(own & (core == 1))
        def _():
            pltpu.make_async_copy(v_ref.at[layer, far_row + row, :, :, lanes], out_ref.at[j], sem).start()

        @pl.when(jnp.logical_not(own))
        def _():
            pltpu.make_async_copy(recv_ref.at[0, row, :, :, lanes], out_ref.at[j], sem).start()

        return carry

    lax.fori_loop(0, n_chunks, step, 0)
    pltpu.make_async_copy(out_ref, out_ref, sem).wait()


def pack(layer, n_chunks, lengths, k_t, v_t, recv):
    return pl.pallas_call(
        functools.partial(pack_kernel, layer, n_chunks),
        out_shape=jax.ShapeDtypeStruct((n_chunks, 2, HEAD_DIM, CHUNK), jnp.bfloat16),
        in_specs=[SMEM, ANY, ANY, ANY], out_specs=VMEM,
        scratch_shapes=[pltpu.SemaphoreType.DMA],
        compiler_params=params(60),
        cost_estimate=pl.CostEstimate(flops=10**9, bytes_accessed=4 * 2**20, transcendentals=0),
    )(lengths, k_t, v_t, recv)


def as_column(row, base):
    wide = jnp.broadcast_to(row[:, base:base + HEAD_DIM].astype(jnp.float32), (HEAD_DIM, HEAD_DIM))
    eye = (lax.broadcasted_iota(jnp.int32, wide.shape, 0) == lax.broadcasted_iota(jnp.int32, wide.shape, 1))
    return jnp.sum(jnp.where(eye, wide, 0.0), axis=1, keepdims=True).astype(jnp.bfloat16)


def spread_mask(group):
    shape = (group, group * HEAD_DIM)
    return lax.broadcasted_iota(jnp.int32, shape, 1) // HEAD_DIM == lax.broadcasted_iota(jnp.int32, shape, 0)


def attend(q_ref, k_buf, v_buf, last, wo_b, wo_copy, mlp_ref, part_o):
    kv_local = k_buf.shape[0]
    width = q_ref.shape[1] // kv_local
    spread = spread_mask(width // HEAD_DIM)
    fold = (lax.broadcasted_iota(jnp.int32, (HEAD_DIM, width), 1) % HEAD_DIM
            == lax.broadcasted_iota(jnp.int32, (HEAD_DIM, width), 0)).astype(jnp.bfloat16)
    part_o[...] = mlp_ref[...]

    def step(head, carry):
        lanes = pl.ds(pl.multiple_of(head * width, width), width)
        q_row = q_ref[:, lanes].astype(jnp.float32)
        q_wide = jnp.where(spread, jnp.broadcast_to(q_row, spread.shape), 0.0).astype(jnp.bfloat16)
        q = lax.dot_general(q_wide, fold, (((1,), (1,)), ((), ())), preferred_element_type=jnp.float32)
        scores = jnp.dot(q.astype(jnp.bfloat16), k_buf[head], preferred_element_type=jnp.float32) * HEAD_DIM ** -0.5
        if last is not None:
            valid = lax.broadcasted_iota(jnp.int32, scores.shape, 1) <= last
            scores = jnp.where(valid, scores, -1e30)
        top = jnp.max(scores, axis=1, keepdims=True)
        expd = jnp.exp(scores - top)
        weights = (expd / jnp.sum(expd, axis=1, keepdims=True)).astype(jnp.bfloat16)
        mixed = lax.dot_general(weights, v_buf[head], (((1,), (1,)), ((), ())), preferred_element_type=jnp.float32)
        wide = jnp.dot(mixed.astype(jnp.bfloat16), fold, preferred_element_type=jnp.float32)
        row = jnp.sum(jnp.where(spread, wide, 0.0), axis=0, keepdims=True).astype(jnp.bfloat16)

        @pl.when(head == 0)
        def _():
            wo_copy.wait()

        row = jnp.broadcast_to(row, (8, width))
        part_o[...] += jnp.dot(row, wo_b[lanes, :], preferred_element_type=jnp.float32)[:1]
        return carry

    lax.fori_loop(0, kv_local, step, 0)


def window_kernel(layer, n_far, aliased, *refs):
    (lengths, q_ref, knew_ref, vnew_ref, mlp_ref, k_ref, v_ref, near_ref, mine_ref, other_ref, wo) = refs[:11]
    refs = refs[13:] if aliased else refs[11:]
    part_o, wk_o, wv_o, k_buf, v_buf, k_far, v_far, wo_b, near_sem, far_sem, wo_sem, out_sem = refs
    row, core, chip = place()
    turn = lengths[row] - WINDOW
    start, _ = far_chunks(lengths[row], chip == 0)
    _, count0 = far_chunks(lengths[2 * chip], chip == 0)
    base = jnp.where(core == 0, 0, count0)
    first = jnp.clip(base, 0, mine_ref.shape[0] - n_far)
    shift = base - first - start
    own = pl.ds(pl.multiple_of(core * SHARD, SHARD), SHARD)
    peer = pl.ds(pl.multiple_of((1 - core) * SHARD, SHARD), SHARD)
    loads = [pltpu.make_async_copy(k_ref.at[layer, row], k_buf.at[:, :, own], near_sem.at[0]),
             pltpu.make_async_copy(v_ref.at[layer, row], v_buf.at[:, :, own], near_sem.at[1]),
             pltpu.make_async_copy(near_ref.at[0, 0], k_buf.at[:, :, peer], near_sem.at[2]),
             pltpu.make_async_copy(near_ref.at[0, 1], v_buf.at[:, :, peer], near_sem.at[3])]
    chunks = pl.ds(first, n_far)

    @pl.when(core == 0)
    def _():
        pltpu.make_async_copy(mine_ref.at[chunks], k_far, far_sem.at[0]).start()
        pltpu.make_async_copy(other_ref.at[chunks], v_far, far_sem.at[1]).start()

    @pl.when(core == 1)
    def _():
        pltpu.make_async_copy(other_ref.at[chunks], k_far, far_sem.at[0]).start()
        pltpu.make_async_copy(mine_ref.at[chunks], v_far, far_sem.at[1]).start()

    for copy in loads:
        copy.start()
    wo_copy = pltpu.make_async_copy(wo.at[layer], wo_b, wo_sem)
    wo_copy.start()
    k_new = [as_column(knew_ref[...], head * HEAD_DIM) for head in range(2)]
    v_new = [as_column(vnew_ref[...], head * HEAD_DIM) for head in range(2)]
    for copy in loads:
        copy.wait()
    pltpu.make_async_copy(mine_ref.at[chunks], k_far, far_sem.at[0]).wait()
    pltpu.make_async_copy(mine_ref.at[chunks], v_far, far_sem.at[1]).wait()

    def step(c, carry):
        lanes = pl.ds(pl.multiple_of(c * CHUNK, CHUNK), CHUNK)
        piece = jnp.clip(c + shift, 0, n_far - 1)
        slots = c * CHUNK + lax.broadcasted_iota(jnp.int32, (HEAD_DIM, CHUNK), 1)
        from_far = jnp.where(chip == 0, turn - slots, slots - turn) > 0
        is_new = slots == turn
        for head in range(2):
            for buf, far, new in ((k_buf, k_far, k_new), (v_buf, v_far, v_new)):
                near = buf[head, :, lanes]
                mixed = jnp.where(from_far, far[piece, head], near)
                buf[head, :, lanes] = jnp.where(is_new, jnp.broadcast_to(new[head], near.shape), mixed)
        return carry

    lax.fori_loop(0, WINDOW // CHUNK, step, 0)
    stores = [pltpu.make_async_copy(k_buf, wk_o.at[layer], out_sem.at[0]),
              pltpu.make_async_copy(v_buf, wv_o.at[layer], out_sem.at[1])]
    for copy in stores:
        copy.start()
    attend(q_ref, k_buf, v_buf, None, wo_b, wo_copy, mlp_ref, part_o)
    for copy in stores:
        copy.wait()


def window(layer, lengths, q, k_new, v_new, mlp, k_t, v_t, near, mine, other, wo, outs):
    n_far = min(WINDOW // CHUNK, mine.shape[0])
    aliased = outs is not None
    args = [lengths, q, k_new, v_new, mlp, k_t, v_t, near, mine, other, wo]
    specs = [SMEM] + [VMEM] * 4 + [ANY] * 6
    aliases = {}
    if aliased:
        args += list(outs)
        specs += [ANY, ANY]
        aliases = {11: 1, 12: 2}
    buf = pltpu.VMEM((2, HEAD_DIM, WINDOW), jnp.bfloat16)
    far = pltpu.VMEM((n_far, 2, HEAD_DIM, CHUNK), jnp.bfloat16)
    out = jax.ShapeDtypeStruct((3, 2, HEAD_DIM, WINDOW), jnp.bfloat16)
    return pl.pallas_call(
        functools.partial(window_kernel, layer, n_far, aliased),
        out_shape=[jax.ShapeDtypeStruct(mlp.shape, jnp.float32), out, out],
        in_specs=specs, out_specs=[VMEM, ANY, ANY],
        scratch_shapes=[buf, buf, far, far, pltpu.VMEM(wo.shape[1:], jnp.bfloat16),
                        pltpu.SemaphoreType.DMA((4,)), pltpu.SemaphoreType.DMA((2,)),
                        pltpu.SemaphoreType.DMA, pltpu.SemaphoreType.DMA((2,))],
        input_output_aliases=aliases,
        compiler_params=params(),
        cost_estimate=pl.CostEstimate(flops=3 * 10**9, bytes_accessed=12 * 2**20, transcendentals=0),
    )(*args)


def global_kernel(layer, lengths, q_ref, knew_ref, vnew_ref, mlp_ref, k_ref, v_ref, near_ref, *refs):
    pieces, (wo, part_o, gk_o, gv_o, k_buf, v_buf, wo_b, load_sem, wo_sem, out_sem) = refs[:4], refs[4:]
    row, core, chip = place()
    last = lengths[row]
    across = row + 2 - 4 * chip
    sources = (row + 1 - 2 * core, across, across + 1 - 2 * core)
    lanes = [pl.ds(pl.multiple_of(shard * SHARD, SHARD), SHARD) for shard in (row,) + sources]
    parts = [k_ref.at[layer, row], v_ref.at[layer, row], near_ref.at[1, 0], near_ref.at[1, 1], *pieces]
    loads = [pltpu.make_async_copy(ref, (k_buf, v_buf)[i % 2].at[:, :, lanes[i // 2]], load_sem.at[i])
             for i, ref in enumerate(parts)]
    for copy in loads:
        copy.start()
    wo_copy = pltpu.make_async_copy(wo.at[layer], wo_b, wo_sem)
    wo_copy.start()
    k_new = [as_column(knew_ref[...], head * HEAD_DIM) for head in range(2)]
    v_new = [as_column(vnew_ref[...], head * HEAD_DIM) for head in range(2)]
    for copy in loads:
        copy.wait()

    def step(c, carry):
        lanes = pl.ds(pl.multiple_of(c * CHUNK, CHUNK), CHUNK)
        slots = c * CHUNK + lax.broadcasted_iota(jnp.int32, (HEAD_DIM, CHUNK), 1)
        for head in range(2):
            for buf, new in ((k_buf, k_new), (v_buf, v_new)):
                near = buf[head, :, lanes]
                kept = jnp.where(slots < last, near, jnp.zeros_like(near))
                buf[head, :, lanes] = jnp.where(slots == last, jnp.broadcast_to(new[head], near.shape), kept)
        return carry

    lax.fori_loop(last // CHUNK, 2 * WINDOW // CHUNK, step, 0)
    stores = [pltpu.make_async_copy(k_buf, gk_o, out_sem.at[0]), pltpu.make_async_copy(v_buf, gv_o, out_sem.at[1])]
    for copy in stores:
        copy.start()
    attend(q_ref, k_buf, v_buf, last, wo_b, wo_copy, mlp_ref, part_o)
    for copy in stores:
        copy.wait()


def global_layer(layer, lengths, q, k_new, v_new, mlp, k_t, v_t, pieces, wo):
    buf = pltpu.VMEM((2, HEAD_DIM, 4 * SHARD), jnp.bfloat16)
    out = jax.ShapeDtypeStruct((2, HEAD_DIM, 4 * SHARD), jnp.bfloat16)
    return pl.pallas_call(
        functools.partial(global_kernel, layer),
        out_shape=[jax.ShapeDtypeStruct(mlp.shape, jnp.float32), out, out],
        in_specs=[SMEM] + [VMEM] * 4 + [ANY] * 8, out_specs=[VMEM, ANY, ANY],
        scratch_shapes=[buf, buf, pltpu.VMEM(wo.shape[1:], jnp.bfloat16), pltpu.SemaphoreType.DMA((8,)),
                        pltpu.SemaphoreType.DMA, pltpu.SemaphoreType.DMA((2,))],
        compiler_params=params(),
        cost_estimate=pl.CostEstimate(flops=3 * 10**9, bytes_accessed=14 * 2**20, transcendentals=0),
        name="global",
    )(lengths, q, k_new, v_new, mlp, k_t, v_t, *pieces, wo)


def run_layers(n_chunks, k_t, v_t, lengths, residual, ln_gain, weights, w_out):
    last = w_out.shape[0] - 1
    (same_k,) = payload(last, (("same", 0),), k_t, v_t)
    same_k = lax.ppermute(same_k, "sp", CROSS)
    streams = []
    for layer in range(last):
        traded = ((layer, True),) if layer < last - 1 else ((layer, True), (last, False))
        far, near = swap(traded, k_t, v_t, 5 + layer)
        packed = pack(layer, n_chunks, lengths, k_t, v_t, far)
        mine = lax.ppermute(packed, "sp", CROSS)
        other = lax.ppermute(mine, "sp", PARTNER)
        streams.append((near, mine, other))
    same_v, cross_k, cross_v = payload(last, (("same", 1), ("cross", 0), ("cross", 1)), k_t, v_t)
    same_v = lax.ppermute(same_v, "sp", CROSS)
    cross_k = lax.ppermute(cross_k, "sp", CROSS_SWAP)
    cross_v = lax.ppermute(cross_v, "sp", CROSS_SWAP)

    my_length = lengths[lax.axis_index("sp")]
    half_dim = HEAD_DIM // 2
    inv_freq = 1.0 / (ROPE_BASE ** (jnp.arange(half_dim, dtype=jnp.float32) * 2.0 / HEAD_DIM))
    angles = my_length.astype(jnp.float32) * inv_freq
    cosine, sine = jnp.cos(angles), jnp.sin(angles)
    cos = jnp.tile(jnp.concatenate([cosine, cosine]), TILE // HEAD_DIM)[None]
    sin = jnp.tile(jnp.concatenate([-sine, sine]), TILE // HEAD_DIM)[None]

    part, outs = None, None
    for layer in range(last + 1):
        q, k_new, v_new, mlp, residual = front(layer, layer < last, residual, part, ln_gain, cos, sin, weights)
        if layer < last:
            part, *outs = window(layer, lengths, q, k_new, v_new, mlp, k_t, v_t, *streams[layer], w_out, outs)
    return (q, k_new, v_new, mlp, residual), (near, same_k, same_v, cross_k, cross_v), outs


def decode(k_t, v_t, lengths, hidden, ln_gain, w_query, w_key, w_value, w_out, w_gate, w_up, w_down):
    weights = (w_query, w_key, w_value, w_gate, w_up, w_down)

    counts = far_chunks(lengths, jnp.arange(4) < 2)[1]
    needed = jnp.maximum(counts[0] + counts[1], counts[2] + counts[3])
    choice = sum((needed > size).astype(jnp.int32) for size in SIZES[:-1])

    def branch(i):
        def run(args):
            return run_layers(SIZES[i], *args)

        return run

    args = (k_t, v_t, lengths, hidden, ln_gain, weights, w_out)
    state, pieces, outs = lax.switch(choice, [branch(i) for i in range(len(SIZES))], args)
    *inputs, residual = state
    part, global_k, global_v = global_layer(w_out.shape[0] - 1, lengths, *inputs, k_t, v_t, pieces, w_out)
    return final(residual, part), outs[0], outs[1], global_k, global_v


SIZES = (34, 50, 64)


def solution(mesh):
    cache_spec = P(None, "dp", "tp", "sp", None)
    row_spec = P(("dp", "sp"), None)
    col_spec = P(None, None, "tp")
    inner_spec = P(None, "tp", None)
    window_spec = P(None, ("dp", "sp"), "tp", None, None)
    global_spec = P(("dp", "sp"), "tp", None, None)
    in_specs = (cache_spec, cache_spec, P("dp"), row_spec, P(None, None), col_spec, col_spec, col_spec, inner_spec, col_spec, col_spec, inner_spec)
    out_specs = (row_spec, window_spec, window_spec, global_spec, global_spec)

    def device_step(k_cache, v_cache, *rest):
        k_t, v_t = jnp.swapaxes(k_cache, 3, 4), jnp.swapaxes(v_cache, 3, 4)
        h, wk, wv, gk, gv = decode(k_t, v_t, *rest)
        turn = lambda x: jnp.swapaxes(x, -1, -2)
        return h, turn(wk)[:, None], turn(wv)[:, None], turn(gk)[None], turn(gv)[None]

    return jax.shard_map(device_step, mesh=mesh, in_specs=in_specs, out_specs=out_specs, check_vma=False)
```

profile of v0, /device:TPU:0, one launch (start us, length us, event | category | flops | bytes accessed | tf_op | source)
XLA Modules:
  0.0 172.8 jit_solution(13427169546591999048)
XLA Ops:
  0.6 0.7 compare_select_fusion
  1.3 0.6 fusion.9
  4.5 153.2 %conditional.1 = (bf16[1,1024]{1,0:T(2,128)(2,1)S(1)}, bf16[1,128]{1,0:T(2,128)(2,1)S(1)}, bf16[1,128]{1,0:T(2,128)(2,1)S(1)}, f32[1,2048]{1,0:T(1,128)S(1)}, bf...) conditional(s32[]{:T(128)} %bitcast.3, (s32[4]{0:T(128)}, ...), branch_computations={%region_0.1_spmd, %region_1.2_spmd, %region_2.3_spmd} | conditional | flops 41000005632 | bytes 355125888 | solution.py:529
  4.5 5.0 %swap.9 = (bf16[1,2,2,64,2048]{4,3,2,1,0:T(8,128)(2,1)}, bf16[1,2,2,64,2048]{4,3,2,1,0:T(8,128)(2,1)}) custom-call(bf16[4,4,2,64,2048]{4,3,2,1,0:T(8,128)(2,1)} %get-tuple-element.86.k_ref.refs_5_, bf16[4,4,2,64,2048]{4,3,2,1,0:T(8,128)(2,1)} %get-tuple-element.87.v_ref.refs_6_), custom_call_target="tpu_custom_call" | custom-call | flops 1000000000 | bytes 4194304 | tf_op jit(solution)/shard_map/cond/branch_0_fun/swap/pallas_call | solution.py:82
  9.6 4.0 %branch_0_fun.11 = bf16[34,2,64,128]{3,2,1,0:T(8,128)(2,1)} custom-call(s32[4]{0:T(128)S(1)} %copy-done.13, bf16[4,4,2,64,2048]{4,3,2,1,0:T(8,128)(2,1)} %get-tuple-element.86.k_ref.refs_5_, bf16[4,4,2,64,2048]{4,3,2,1,0:T(8,128)(2,1)} %get-tuple-element.87.v_ref.refs_6_, bf16[1,2,2,64,2048]{4,3,2,1,0:T(8,128)(2,1)} %get-tuple-element.89.recv_ref), custom_call_target="tpu_custom_call" | custom-call | flops 1000000000 | bytes 4194304 | tf_op jit(solution)/shard_map/cond/branch_0_fun/pallas_call | solution.py:284
  13.6 1.9 %collective-permute-start = (bf16[34,2,64,128]{3,2,1,0:T(8,128)(2,1)}, bf16[34,2,64,128]{3,2,1,0:T(8,128)(2,1)S(1)}, u32[]{:S(2)}, u32[]{:S(2)}) collective-permute-start(bf16[34,2,64,128]{3,2,1,0:T(8,128)(2,1)} %branch_0_fun.11), channel_id=1, source_target_pairs={{0,2},{2,0},{1,3},{3,1},{4,6},{6,4},{5,7},{7,5}} | collective-permute-start | bytes 3342344 | tf_op jit(solution)/shard_map/cond/branch_0_fun/ppermute | solution.py:491
  15.5 4.6 %swap.10 = (bf16[1,2,2,64,2048]{4,3,2,1,0:T(8,128)(2,1)}, bf16[1,2,2,64,2048]{4,3,2,1,0:T(8,128)(2,1)}) custom-call(bf16[4,4,2,64,2048]{4,3,2,1,0:T(8,128)(2,1)} %get-tuple-element.86.k_ref.refs_5_, bf16[4,4,2,64,2048]{4,3,2,1,0:T(8,128)(2,1)} %get-tuple-element.87.v_ref.refs_6_), custom_call_target="tpu_custom_call" | custom-call | flops 1000000000 | bytes 4194304 | tf_op jit(solution)/shard_map/cond/branch_0_fun/swap/pallas_call | solution.py:82
  20.1 4.0 %branch_0_fun.14 = bf16[34,2,64,128]{3,2,1,0:T(8,128)(2,1)} custom-call(s32[4]{0:T(128)S(1)} %copy-done.13, bf16[4,4,2,64,2048]{4,3,2,1,0:T(8,128)(2,1)} %get-tuple-element.86.k_ref.refs_5_, bf16[4,4,2,64,2048]{4,3,2,1,0:T(8,128)(2,1)} %get-tuple-element.87.v_ref.refs_6_, bf16[1,2,2,64,2048]{4,3,2,1,0:T(8,128)(2,1)} %get-tuple-element.98.recv_ref), custom_call_target="tpu_custom_call" | custom-call | flops 1000000000 | bytes 4194304 | tf_op jit(solution)/shard_map/cond/branch_0_fun/pallas_call | solution.py:284
  24.1 6.1 %swap.11 = (bf16[2,2,2,64,2048]{4,3,2,1,0:T(8,128)(2,1)}, bf16[2,2,2,64,2048]{4,3,2,1,0:T(8,128)(2,1)}) custom-call(bf16[4,4,2,64,2048]{4,3,2,1,0:T(8,128)(2,1)} %get-tuple-element.86.k_ref.refs_5_, bf16[4,4,2,64,2048]{4,3,2,1,0:T(8,128)(2,1)} %get-tuple-element.87.v_ref.refs_6_), custom_call_target="tpu_custom_call" | custom-call | flops 1000000000 | bytes 4194304 | tf_op jit(solution)/shard_map/cond/branch_0_fun/swap/pallas_call | solution.py:82
  30.2 4.0 %branch_0_fun.17 = bf16[34,2,64,128]{3,2,1,0:T(8,128)(2,1)} custom-call(s32[4]{0:T(128)S(1)} %copy-done.13, bf16[4,4,2,64,2048]{4,3,2,1,0:T(8,128)(2,1)} %get-tuple-element.86.k_ref.refs_5_, bf16[4,4,2,64,2048]{4,3,2,1,0:T(8,128)(2,1)} %get-tuple-element.87.v_ref.refs_6_, bf16[2,2,2,64,2048]{4,3,2,1,0:T(8,128)(2,1)} %get-tuple-element.108.recv_ref), custom_call_target="tpu_custom_call" | custom-call | flops 1000000000 | bytes 4194304 | tf_op jit(solution)/shard_map/cond/branch_0_fun/pallas_call | solution.py:284
  34.2 1.1 collective-permute-start.4
  35.3 5.9 %collective-permute-done.refs_8_ = bf16[34,2,64,128]{3,2,1,0:T(8,128)(2,1)S(1)} collective-permute-done((bf16[34,2,64,128]{3,2,1,0:T(8,128)(2,1)}, bf16[34,2,64,128]{3,2,1,0:T(8,128)(2,1)S(1)}, u32[]{:S(2)}, u32[]{:S(2)}) %collective-permute-start) | collective-permute-done | bytes 1114144 | tf_op jit(solution)/shard_map/cond/branch_0_fun/ppermute | solution.py:491
  41.2 1.8 %payload.6 = bf16[2,64,2048]{2,1,0:T(8,128)(2,1)} custom-call(bf16[4,4,2,64,2048]{4,3,2,1,0:T(8,128)(2,1)} %get-tuple-element.86.k_ref.refs_5_, bf16[4,4,2,64,2048]{4,3,2,1,0:T(8,128)(2,1)} %get-tuple-element.87.v_ref.refs_6_), custom_call_target="tpu_custom_call" | custom-call | flops 1000000000 | bytes 1048576 | tf_op jit(solution)/shard_map/cond/branch_0_fun/payload/pallas_call | solution.py:107
  43.1 1.9 %collective-permute-start.6 = (bf16[2,64,2048]{2,1,0:T(8,128)(2,1)}, bf16[2,64,2048]{2,1,0:T(8,128)(2,1)}, u32[]{:S(2)}, u32[]{:S(2)}) collective-permute-start(bf16[2,64,2048]{2,1,0:T(8,128)(2,1)} %payload.6), channel_id=1, source_target_pairs={{0,2},{2,0},{1,3},{3,1},{4,6},{6,4},{5,7},{7,5}} | collective-permute-start | bytes 1572872 | tf_op jit(solution)/shard_map/cond/branch_0_fun/ppermute | solution.py:485
  45.0 2.6 %payload.7 = (bf16[2,64,2048]{2,1,0:T(8,128)(2,1)}, bf16[2,64,2048]{2,1,0:T(8,128)(2,1)}, bf16[2,64,2048]{2,1,0:T(8,128)(2,1)}) custom-call(bf16[4,4,2,64,2048]{4,3,2,1,0:T(8,128)(2,1)} %get-tuple-element.86.k_ref.refs_5_, bf16[4,4,2,64,2048]{4,3,2,1,0:T(8,128)(2,1)} %get-tuple-element.87.v_ref.refs_6_), custom_call_target="tpu_custom_call" | custom-call | flops 1000000000 | bytes 3145728 | tf_op jit(solution)/shard_map/cond/branch_0_fun/payload/pallas_call | solution.py:107
  47.6 0.1 collective-permute-start.7
  47.8 0.6 dynamic_slice.6
  49.1 0.1 tile.9.refs_2_.refs_3_
  49.5 15.6 %collective-permute-done.2.refs_8_ = bf16[34,2,64,128]{3,2,1,0:T(8,128)(2,1)S(1)} collective-permute-done((bf16[34,2,64,128]{3,2,1,0:T(8,128)(2,1)}, bf16[34,2,64,128]{3,2,1,0:T(8,128)(2,1)S(1)}, u32[]{:S(2)}, u32[]{:S(2)}) %collective-permute-start.2) | collective-permute-done | bytes 1114144 | tf_op jit(solution)/shard_map/cond/branch_0_fun/ppermute | solution.py:491
  65.2 17.2 %branch_0_fun.10 = (bf16[1,1024]{1,0:T(2,128)(2,1)S(1)}, bf16[1,128]{1,0:T(2,128)(2,1)S(1)}, bf16[1,128]{1,0:T(2,128)(2,1)S(1)}, f32[1,2048]{1,0:T(1,128)S(1)}, bf16[1,2048]{1,0:T(2,128)(2,1)S(1)}) custom-call(bf16[1,2048]{1,0:T(2,128)(2,1)S(1)} %copy-done.16, bf16[4,2048]{1,0:T(4,128)(2,1)S(1)} %copy-done.10, f32[1,256]{1,0:T(1,128)S(1)} %tile.9.refs_2_.refs_3_, ...), custom_call_target="tpu_custom_call" | custom-call | flops 6000000000 | bytes 40000000 | tf_op jit(solution)/shard_map/cond/branch_0_fun/pallas_call | solution.py:224
  82.4 6.6 %collective-permute-done.4.refs_8_ = bf16[34,2,64,128]{3,2,1,0:T(8,128)(2,1)S(1)} collective-permute-done((bf16[34,2,64,128]{3,2,1,0:T(8,128)(2,1)}, bf16[34,2,64,128]{3,2,1,0:T(8,128)(2,1)S(1)}, u32[]{:S(2)}, u32[]{:S(2)}) %collective-permute-start.4) | collective-permute-done | bytes 1114144 | tf_op jit(solution)/shard_map/cond/branch_0_fun/ppermute | solution.py:491
  89.0 2.0 %collective-permute-start.5 = (bf16[34,2,64,128]{3,2,1,0:T(8,128)(2,1)S(1)}, bf16[34,2,64,128]{3,2,1,0:T(8,128)(2,1)S(1)}, u32[]{:S(2)}, u32[]{:S(2)}) collective-permute-start(bf16[34,2,64,128]{3,2,1,0:T(8,128)(2,1)S(1)} %collective-permute-done.4.refs_8_), channel_id=1, source_target_pairs={{0,1},{1,0},{2,3},{3,2},{4,5},{5,4},{6,7},{7,6}} | collective-permute-start | bytes 3342344 | tf_op jit(solution)/shard_map/cond/branch_0_fun/ppermute | solution.py:492
  91.0 6.2 %branch_0_fun.12 = (f32[1,2048]{1,0:T(1,128)S(1)}, bf16[3,2,64,4096]{3,2,1,0:T(8,128)(2,1)}, bf16[3,2,64,4096]{3,2,1,0:T(8,128)(2,1)}) custom-call(s32[4]{0:T(128)S(1)} %copy-done.13, bf16[1,1024]{1,0:T(2,128)(2,1)S(1)} %get-tuple-element.82.refs_1_, bf16[1,128]{1,0:T(2,128)(2,1)S(1)} %get-tuple-element.83.refs_2_, ...), custom_call_target="tpu_custom_call" | custom-call | flops 3000000000 | bytes 12582912 | tf_op jit(solution)/shard_map/cond/branch_0_fun/pallas_call | solution.py:416
  97.3 16.3 %branch_0_fun.13 = (bf16[1,1024]{1,0:T(2,128)(2,1)S(1)}, bf16[1,128]{1,0:T(2,128)(2,1)S(1)}, bf16[1,128]{1,0:T(2,128)(2,1)S(1)}, f32[1,2048]{1,0:T(1,128)S(1)}, bf16[1,2048]{1,0:T(2,128)(2,1)S(1)}) custom-call(bf16[1,2048]{1,0:T(2,128)(2,1)S(1)} %get-tuple-element.81.refs_0_, f32[1,2048]{1,0:T(1,128)S(1)} %get-tuple-element.91.refs_1_, ...), custom_call_target="tpu_custom_call" | custom-call | flops 6000000000 | bytes 40000000 | tf_op jit(solution)/shard_map/cond/branch_0_fun/pallas_call | solution.py:224
  113.7 5.4 %branch_0_fun.15 = (f32[1,2048]{1,0:T(1,128)S(1)}, bf16[3,2,64,4096]{3,2,1,0:T(8,128)(2,1)}, bf16[3,2,64,4096]{3,2,1,0:T(8,128)(2,1)}) custom-call(s32[4]{0:T(128)S(1)} %copy-done.13, bf16[1,1024]{1,0:T(2,128)(2,1)S(1)} %get-tuple-element.93.refs_1_, bf16[1,128]{1,0:T(2,128)(2,1)S(1)} %get-tuple-element.94.refs_2_, ...), custom_call_target="tpu_custom_call", output_to_operand_aliasing={{1}: (11, {}), {2}: (12, {})} | custom-call | flops 3000000000 | bytes 12582912 | tf_op jit(solution)/shard_map/cond/branch_0_fun/pallas_call | solution.py:416
  119.1 16.1 %branch_0_fun.16 = (bf16[1,1024]{1,0:T(2,128)(2,1)S(1)}, bf16[1,128]{1,0:T(2,128)(2,1)S(1)}, bf16[1,128]{1,0:T(2,128)(2,1)S(1)}, f32[1,2048]{1,0:T(1,128)S(1)}, bf16[1,2048]{1,0:T(2,128)(2,1)S(1)}) custom-call(bf16[1,2048]{1,0:T(2,128)(2,1)S(1)} %get-tuple-element.92.refs_0_, f32[1,2048]{1,0:T(1,128)S(1)} %get-tuple-element.101.refs_1_, ...), custom_call_target="tpu_custom_call" | custom-call | flops 6000000000 | bytes 40000000 | tf_op jit(solution)/shard_map/cond/branch_0_fun/pallas_call | solution.py:224
  135.3 6.4 %branch_0_fun.18 = (f32[1,2048]{1,0:T(1,128)S(1)}, bf16[3,2,64,4096]{3,2,1,0:T(8,128)(2,1)}, bf16[3,2,64,4096]{3,2,1,0:T(8,128)(2,1)}) custom-call(s32[4]{0:T(128)S(1)} %copy-done.13, bf16[1,1024]{1,0:T(2,128)(2,1)S(1)} %get-tuple-element.103.refs_1_, bf16[1,128]{1,0:T(2,128)(2,1)S(1)} %get-tuple-element.104.refs_2_, ...), custom_call_target="tpu_custom_call", output_to_operand_aliasing={{1}: (11, {}), {2}: (12, {})} | custom-call | flops 3000000000 | bytes 12582912 | tf_op jit(solution)/shard_map/cond/branch_0_fun/pallas_call | solution.py:416
  141.7 15.8 %branch_0_fun.19 = (bf16[1,1024]{1,0:T(2,128)(2,1)S(1)}, bf16[1,128]{1,0:T(2,128)(2,1)S(1)}, bf16[1,128]{1,0:T(2,128)(2,1)S(1)}, f32[1,2048]{1,0:T(1,128)S(1)}, bf16[1,2048]{1,0:T(2,128)(2,1)S(1)}) custom-call(bf16[1,2048]{1,0:T(2,128)(2,1)S(1)} %get-tuple-element.102.refs_0_, f32[1,2048]{1,0:T(1,128)S(1)} %get-tuple-element.111.refs_1_, ...), custom_call_target="tpu_custom_call" | custom-call | flops 6000000000 | bytes 40000000 | tf_op jit(solution)/shard_map/cond/branch_0_fun/pallas_call | solution.py:224
  157.7 7.7 %global.1 = (f32[1,2048]{1,0:T(1,128)S(1)}, bf16[2,64,8192]{2,1,0:T(8,128)(2,1)}, bf16[2,64,8192]{2,1,0:T(8,128)(2,1)}) custom-call(s32[4]{0:T(128)} %lengths.1, bf16[1,1024]{1,0:T(2,128)(2,1)S(1)} %get-tuple-element.243.q_ref, bf16[1,128]{1,0:T(2,128)(2,1)S(1)} %get-tuple-element.244.knew_ref, bf16[1,128]{1,0:T(2,128)(2,1)S(1)} %get-tuple-element.245.vnew_ref, ...), custom_call_target="tpu_custom_call" | custom-call | flops 3000000000 | bytes 14680064 | tf_op jit(solution)/shard_map/global/pallas_call | solution.py:470
  165.4 0.6 copy-done.6
  166.0 5.5 %final.1 = bf16[1,2048]{1,0:T(2,128)(2,1)} custom-call(bf16[1,2048]{1,0:T(2,128)(2,1)S(1)} %get-tuple-element.242.h_ref, f32[1,2048]{1,0:T(1,128)} %copy-done.6), custom_call_target="tpu_custom_call" | custom-call | tf_op jit(solution)/shard_map/final/pallas_call | solution.py:241
  171.5 1.3 copy.78
  (42 shorter events, 0.5 us)
Async XLA Ops:
  4.5 5.1 %copy-start.13 = (s32[4]{0:T(128)S(1)}, s32[4]{0:T(128)}, u32[]{:S(2)}) copy-start(s32[4]{0:T(128)} %get-tuple-element.74.lengths.refs_0_) | copy-start | bytes 52 | tf_op jit(solution)/shard_map/cond
  13.6 27.7 %collective-permute-start = (bf16[34,2,64,128]{3,2,1,0:T(8,128)(2,1)}, bf16[34,2,64,128]{3,2,1,0:T(8,128)(2,1)S(1)}, u32[]{:S(2)}, u32[]{:S(2)}) collective-permute-start(bf16[34,2,64,128]{3,2,1,0:T(8,128)(2,1)} %branch_0_fun.11), channel_id=1, source_target_pairs={{0,2},{2,0},{1,3},{3,1},{4,6},{6,4},{5,7},{7,5}} | collective-permute-start | bytes 3342344 | tf_op jit(solution)/shard_map/cond/branch_0_fun/ppermute | solution.py:491
  24.0 41.1 %collective-permute-start.2 = (bf16[34,2,64,128]{3,2,1,0:T(8,128)(2,1)}, bf16[34,2,64,128]{3,2,1,0:T(8,128)(2,1)S(1)}, u32[]{:S(2)}, u32[]{:S(2)}) collective-permute-start(bf16[34,2,64,128]{3,2,1,0:T(8,128)(2,1)} %branch_0_fun.14), channel_id=1, source_target_pairs={{0,2},{2,0},{1,3},{3,1},{4,6},{6,4},{5,7},{7,5}} | collective-permute-start | bytes 3342344 | tf_op jit(solution)/shard_map/cond/branch_0_fun/ppermute | solution.py:491
  34.2 54.8 %collective-permute-start.4 = (bf16[34,2,64,128]{3,2,1,0:T(8,128)(2,1)}, bf16[34,2,64,128]{3,2,1,0:T(8,128)(2,1)S(1)}, u32[]{:S(2)}, u32[]{:S(2)}) collective-permute-start(bf16[34,2,64,128]{3,2,1,0:T(8,128)(2,1)} %branch_0_fun.17), channel_id=1, source_target_pairs={{0,2},{2,0},{1,3},{3,1},{4,6},{6,4},{5,7},{7,5}} | collective-permute-start | bytes 3342344 | tf_op jit(solution)/shard_map/cond/branch_0_fun/ppermute | solution.py:491
  41.2 47.8 %collective-permute-start.1 = (bf16[34,2,64,128]{3,2,1,0:T(8,128)(2,1)S(1)}, bf16[34,2,64,128]{3,2,1,0:T(8,128)(2,1)}, u32[]{:S(2)}, u32[]{:S(2)}) collective-permute-start(bf16[34,2,64,128]{3,2,1,0:T(8,128)(2,1)S(1)} %collective-permute-done.refs_8_), channel_id=1, source_target_pairs={{0,1},{1,0},{2,3},{3,2},{4,5},{5,4},{6,7},{7,6}} | collective-permute-start | bytes 3342344 | tf_op jit(solution)/shard_map/cond/branch_0_fun/ppermute | solution.py:492
  43.1 22.0 %copy-start.10 = (bf16[4,2048]{1,0:T(4,128)(2,1)S(1)}, bf16[4,2048]{1,0:T(4,128)(2,1)}, u32[]{:S(2)}) copy-start(bf16[4,2048]{1,0:T(4,128)(2,1)} %get-tuple-element.73.refs_1_.refs_2_) | copy-start | bytes 49156 | tf_op jit(solution)/shard_map/cond
  43.1 22.0 %copy-start.16 = (bf16[1,2048]{1,0:T(2,128)(2,1)S(1)}, bf16[1,2048]{1,0:T(2,128)(2,1)}, u32[]{:S(2)}) copy-start(bf16[1,2048]{1,0:T(2,128)(2,1)} %get-tuple-element.72.refs_0_) | copy-start | bytes 12292 | tf_op jit(solution)/shard_map/cond
  43.1 114.3 %collective-permute-start.6 = (bf16[2,64,2048]{2,1,0:T(8,128)(2,1)}, bf16[2,64,2048]{2,1,0:T(8,128)(2,1)}, u32[]{:S(2)}, u32[]{:S(2)}) collective-permute-start(bf16[2,64,2048]{2,1,0:T(8,128)(2,1)} %payload.6), channel_id=1, source_target_pairs={{0,2},{2,0},{1,3},{3,1},{4,6},{6,4},{5,7},{7,5}} | collective-permute-start | bytes 1572872 | tf_op jit(solution)/shard_map/cond/branch_0_fun/ppermute | solution.py:485
  47.6 109.8 %collective-permute-start.7 = (bf16[2,64,2048]{2,1,0:T(8,128)(2,1)}, bf16[2,64,2048]{2,1,0:T(8,128)(2,1)}, u32[]{:S(2)}, u32[]{:S(2)}) collective-permute-start(bf16[2,64,2048]{2,1,0:T(8,128)(2,1)} %get-tuple-element.117), channel_id=1, source_target_pairs={{0,2},{2,0},{1,3},{3,1},{4,6},{6,4},{5,7},{7,5}} | collective-permute-start | bytes 1572872 | tf_op jit(solution)/shard_map/cond/branch_0_fun/ppermute | solution.py:495
  65.1 48.5 %collective-permute-start.3 = (bf16[34,2,64,128]{3,2,1,0:T(8,128)(2,1)S(1)}, bf16[34,2,64,128]{3,2,1,0:T(8,128)(2,1)S(1)}, u32[]{:S(2)}, u32[]{:S(2)}) collective-permute-start(bf16[34,2,64,128]{3,2,1,0:T(8,128)(2,1)S(1)} %collective-permute-done.2.refs_8_), channel_id=1, source_target_pairs={{0,1},{1,0},{2,3},{3,2},{4,5},{5,4},{6,7},{7,6}} | collective-permute-start | bytes 3342344 | tf_op jit(solution)/shard_map/cond/branch_0_fun/ppermute | solution.py:492
  65.1 25.9 %slice-start = ((s8[8388608]{0:T(1024)(128)(4,1)}), s8[4194304]{0:T(1024)(128)(4,1)S(1)}, s32[]{:S(2)}) async-start(s8[8388608]{0:T(1024)(128)(4,1)} %bitcast.22), calls=%async_computation | async-start | bytes 8388608 | tf_op jit(solution)/shard_map/cond
  65.1 25.9 %slice-start.6 = ((s8[8388608]{0:T(1024)(128)(4,1)}), s8[4194304]{0:T(1024)(128)(4,1)S(1)}, s32[]{:S(2)}) async-start(s8[8388608]{0:T(1024)(128)(4,1)} %bitcast.32), calls=%async_computation.6 | async-start | bytes 8388608 | tf_op jit(solution)/shard_map/cond
  65.1 25.9 %copy-start.3 = (bf16[1,2,2,64,2048]{4,3,2,1,0:T(8,128)(2,1)S(1)}, bf16[1,2,2,64,2048]{4,3,2,1,0:T(8,128)(2,1)}, u32[]{:S(2)}) copy-start(bf16[1,2,2,64,2048]{4,3,2,1,0:T(8,128)(2,1)} %get-tuple-element.88.refs_7_) | copy-start | bytes 3145732 | tf_op jit(solution)/shard_map/cond
  65.1 25.9 %slice-start.1 = ((s8[8388608]{0:T(1024)(128)(4,1)}), s8[4194304]{0:T(1024)(128)(4,1)S(1)}, s32[]{:S(2)}) async-start(s8[8388608]{0:T(1024)(128)(4,1)} %bitcast.22), calls=%async_computation.1 | async-start | bytes 8388608 | tf_op jit(solution)/shard_map/cond
  65.1 25.9 %slice-start.7 = ((s8[8388608]{0:T(1024)(128)(4,1)}), s8[4194304]{0:T(1024)(128)(4,1)S(1)}, s32[]{:S(2)}) async-start(s8[8388608]{0:T(1024)(128)(4,1)} %bitcast.32), calls=%async_computation.7 | async-start | bytes 8388608 | tf_op jit(solution)/shard_map/cond
  89.0 68.5 %collective-permute-start.8 = (bf16[2,64,2048]{2,1,0:T(8,128)(2,1)}, bf16[2,64,2048]{2,1,0:T(8,128)(2,1)}, u32[]{:S(2)}, u32[]{:S(2)}) collective-permute-start(bf16[2,64,2048]{2,1,0:T(8,128)(2,1)} %get-tuple-element.118), channel_id=1, source_target_pairs={{0,3},{3,0},{1,2},{2,1},{4,7},{7,4},{5,6},{6,5}} | collective-permute-start | bytes 1572872 | tf_op jit(solution)/shard_map/cond/branch_0_fun/ppermute | solution.py:496
  89.0 46.3 %collective-permute-start.5 = (bf16[34,2,64,128]{3,2,1,0:T(8,128)(2,1)S(1)}, bf16[34,2,64,128]{3,2,1,0:T(8,128)(2,1)S(1)}, u32[]{:S(2)}, u32[]{:S(2)}) collective-permute-start(bf16[34,2,64,128]{3,2,1,0:T(8,128)(2,1)S(1)} %collective-permute-done.4.refs_8_), channel_id=1, source_target_pairs={{0,1},{1,0},{2,3},{3,2},{4,5},{5,4},{6,7},{7,6}} | collective-permute-start | bytes 3342344 | tf_op jit(solution)/shard_map/cond/branch_0_fun/ppermute | solution.py:492
  97.3 16.4 %copy-start = (bf16[1,2,2,64,2048]{4,3,2,1,0:T(8,128)(2,1)S(1)}, bf16[1,2,2,64,2048]{4,3,2,1,0:T(8,128)(2,1)}, u32[]{:S(2)}) copy-start(bf16[1,2,2,64,2048]{4,3,2,1,0:T(8,128)(2,1)} %get-tuple-element.97.refs_7_) | copy-start | bytes 3145732 | tf_op jit(solution)/shard_map/cond
  113.6 43.9 %collective-permute-start.9 = (bf16[2,64,2048]{2,1,0:T(8,128)(2,1)}, bf16[2,64,2048]{2,1,0:T(8,128)(2,1)}, u32[]{:S(2)}, u32[]{:S(2)}) collective-permute-start(bf16[2,64,2048]{2,1,0:T(8,128)(2,1)} %get-tuple-element.119), channel_id=1, source_target_pairs={{0,3},{3,0},{1,2},{2,1},{4,7},{7,4},{5,6},{6,5}} | collective-permute-start | bytes 1572872 | tf_op jit(solution)/shard_map/cond/branch_0_fun/ppermute | solution.py:497
  113.7 5.4 %copy-start.7 = (bf16[4,2048,128]{2,1,0:T(8,128)(2,1)S(1)}, bf16[4,2048,128]{2,1,0:T(8,128)(2,1)}, u32[]{:S(2)}) copy-start(bf16[4,2048,128]{2,1,0:T(8,128)(2,1)} %get-tuple-element.76.refs_5_.refs_6_) | copy-start | bytes 6291460 | tf_op jit(solution)/shard_map/cond
  165.4 0.6 copy-start.6
where the time goes:
time: 174 us; the launch traced here: 173 us
  Pallas kernels  129 us (74%)
  waiting for transfers between devices  28.2 us (16%)
  starting transfers between devices  7.16 us (4%)
  local copies, waits for them, and re-layouts  3.3 us (2%)
  between operations  3.27 us (2%)
    pallas_call x4, Pallas kernels, front(): pl.pallas_call(functools.partial(front_kernel, layer, sliding, exchange),...  65.4 us
    ppermute x3, waiting for transfers between devices, run_layers(): mine = lax.ppermute(packed, 'sp', CROSS)  28.2 us
    pallas_call x3, Pallas kernels, window(): pl.pallas_call(functools.partial(window_kernel, layer, n_far, aliased), o...  18 us
    pallas_call x3, Pallas kernels, swap(): pl.pallas_call(functools.partial(swap_kernel, layers), out_shape=[block,...  15.7 us
    pallas_call x3, Pallas kernels, pack(): pl.pallas_call(functools.partial(pack_kernel, layer, n_chunks), out_shape...  12 us
    pallas_call x1, Pallas kernels, global_layer(): pl.pallas_call(functools.partial(global_kernel, layer), out_shape=[jax.Sh...  7.65 us
    pallas_call x1, Pallas kernels, final(): pl.pallas_call(final_kernel, out_shape=jax.ShapeDtypeStruct(h.shape, jnp....  5.47 us
    pallas_call x2, Pallas kernels, payload(): pl.pallas_call(functools.partial(payload_kernel, layer, picks), out_shape...  4.43 us
  transfers between devices with their start and end apart: 10, of which 3 were waited for; matrix products, arithmetic and copies ran while one was open for 1% of the time, Pallas kernels for 62%

commit v1 on v0

v1 whole, which is shorter than its diff:
```python
import functools

import jax
import jax.numpy as jnp
from jax import lax
from jax.experimental import pallas as pl
from jax.experimental.pallas import tpu as pltpu
from jax.sharding import PartitionSpec as P


WINDOW = 4096
ROPE_BASE = 50000
NORM_EPS = 1e-5
SHARD = 2048
CHUNK = 128
HEAD_DIM = 64
DEPTH = 5
TILE = 256
CROSS = [(0, 2), (2, 0), (1, 3), (3, 1)]
CROSS_SWAP = [(0, 3), (3, 0), (1, 2), (2, 1)]
PARTNER = [(0, 1), (1, 0), (2, 3), (3, 2)]


VMEM = pl.BlockSpec(memory_space=pltpu.VMEM)
SMEM = pl.BlockSpec(memory_space=pltpu.SMEM)
ANY = pl.BlockSpec(memory_space=pltpu.HBM)
EITHER = pl.BlockSpec(memory_space=pl.ANY)


def params(mib=52, **extra):
    return pltpu.CompilerParams(vmem_limit_bytes=mib * 2**20, **extra)


def place():
    sp = lax.axis_index("sp")
    return sp, lax.rem(sp, 2), sp // 2


def far_chunks(length, on_first_chip):
    turn = length - WINDOW
    start = jnp.where(on_first_chip, 0, (turn + 1) // CHUNK)
    count = jnp.where(on_first_chip, (turn + CHUNK - 1) // CHUNK, WINDOW // CHUNK - (turn + 1) // CHUNK)
    return start, count


def swap_kernel(layers, k_ref, v_ref, far_o, near_o, send_sem, recv_sem):
    sp, core, chip = place()
    peer = sp + 1 - 2 * core
    barrier = pltpu.get_barrier_semaphore()
    pl.semaphore_signal(barrier, inc=1, device_id={"sp": peer}, device_id_type=pl.DeviceIdType.MESH)
    pl.semaphore_wait(barrier, 1)
    far_rows = pl.ds(2 * (1 - chip), 2)

    def send(src, dst, i):
        return pltpu.make_async_remote_copy(
            src_ref=src, dst_ref=dst, send_sem=send_sem.at[i], recv_sem=recv_sem.at[i],
            device_id={"sp": peer}, device_id_type=pl.DeviceIdType.MESH)

    copies = []
    for i, (layer, sliding) in enumerate(layers):
        if sliding:
            @pl.when(core == 0)
            def _(layer=layer, i=i):
                send(v_ref.at[layer, far_rows], far_o.at[i], 3 * i).start()

            @pl.when(core == 1)
            def _(layer=layer, i=i):
                send(k_ref.at[layer, far_rows], far_o.at[i], 3 * i).start()

            copies.append(send(k_ref.at[layer, far_rows], far_o.at[i], 3 * i))
        pair = [send(k_ref.at[layer, peer], near_o.at[i, 0], 3 * i + 1),
                send(v_ref.at[layer, peer], near_o.at[i, 1], 3 * i + 2)]
        for copy in pair:
            copy.start()
        copies += pair
    for copy in copies:
        copy.wait()


def swap(layers, k_t, v_t, collective_id):
    n = len(layers)
    block = jax.ShapeDtypeStruct((n, 2, 2, HEAD_DIM, SHARD), jnp.bfloat16)
    return pl.pallas_call(
        functools.partial(swap_kernel, layers),
        out_shape=[block, block],
        in_specs=[ANY, ANY], out_specs=[ANY, ANY],
        scratch_shapes=[pltpu.SemaphoreType.DMA((3 * n,)), pltpu.SemaphoreType.DMA((3 * n,))],
        compiler_params=params(60, collective_id=collective_id, has_side_effects=True),
        cost_estimate=pl.CostEstimate(flops=10**9, bytes_accessed=4 * 2**20, transcendentals=0),
        name="swap",
    )(k_t, v_t)


def pack_kernel(layer, n_chunks, lengths, k_ref, v_ref, recv_ref, out_ref, sem):
    _, core, chip = place()
    far_row = 2 * (1 - chip)
    start0, count0 = far_chunks(lengths[far_row], chip == 1)
    start1, _ = far_chunks(lengths[far_row + 1], chip == 1)
    per_shard = SHARD // CHUNK

    def step(j, carry):
        second = j >= count0
        row = jnp.where(second, 1, 0)
        piece = jnp.clip(jnp.where(second, start1 + j - count0, start0 + j), 0, 2 * per_shard - 1)
        own = (piece // per_shard) == core
        lanes = pl.ds(pl.multiple_of(lax.rem(piece, per_shard) * CHUNK, CHUNK), CHUNK)

        @pl.when(own & (core == 0))
        def _():
            pltpu.make_async_copy(k_ref.at[layer, far_row + row, :, :, lanes], out_ref.at[j], sem).start()

        @pl.when(own & (core == 1))
        def _():
            pltpu.make_async_copy(v_ref.at[layer, far_row + row, :, :, lanes], out_ref.at[j], sem).start()

        @pl.when(jnp.logical_not(own))
        def _():
            pltpu.make_async_copy(recv_ref.at[0, row, :, :, lanes], out_ref.at[j], sem).start()

        return carry

    lax.fori_loop(0, n_chunks, step, 0)
    pltpu.make_async_copy(out_ref, out_ref, sem).wait()


def pack(layer, n_chunks, lengths, k_t, v_t, recv):
    return pl.pallas_call(
        functools.partial(pack_kernel, layer, n_chunks),
        out_shape=jax.ShapeDtypeStruct((n_chunks, 2, HEAD_DIM, CHUNK), jnp.bfloat16),
        in_specs=[SMEM, ANY, ANY, ANY], out_specs=VMEM,
        scratch_shapes=[pltpu.SemaphoreType.DMA],
        compiler_params=params(60),
        cost_estimate=pl.CostEstimate(flops=10**9, bytes_accessed=4 * 2**20, transcendentals=0),
    )(lengths, k_t, v_t, recv)


def payload_kernel(layer, picks, k_ref, v_ref, *refs):
    sp, core, chip = place()
    rows = {"same": sp + 2 - 4 * chip, "cross": 2 * (1 - chip) + 1 - core}
    sems = refs[-1]
    copies = [pltpu.make_async_copy((k_ref, v_ref)[which].at[layer, rows[kind]], out, sems.at[i])
              for i, ((kind, which), out) in enumerate(zip(picks, refs))]
    for copy in copies:
        copy.start()
    for copy in copies:
        copy.wait()


def payload(layer, picks, k_t, v_t):
    block = jax.ShapeDtypeStruct((2, HEAD_DIM, SHARD), jnp.bfloat16)
    return pl.pallas_call(
        functools.partial(payload_kernel, layer, picks),
        out_shape=[block] * len(picks),
        in_specs=[ANY, ANY], out_specs=[VMEM] * len(picks),
        scratch_shapes=[pltpu.SemaphoreType.DMA((len(picks),))],
        compiler_params=params(60),
        cost_estimate=pl.CostEstimate(flops=10**9, bytes_accessed=len(picks) * 2**20, transcendentals=0),
        name="payload",
    )(k_t, v_t)


def greet_peer():
    pl.semaphore_signal(pltpu.get_barrier_semaphore(), inc=1, device_id={"tp": 1 - lax.axis_index("tp")},
                        device_id_type=pl.DeviceIdType.MESH)


def swap_partials(part_ref, other_ref, sems):
    pl.semaphore_wait(pltpu.get_barrier_semaphore(), 1)
    copy = pltpu.make_async_remote_copy(
        src_ref=part_ref, dst_ref=other_ref, send_sem=sems.at[0], recv_sem=sems.at[1],
        device_id={"tp": 1 - lax.axis_index("tp")}, device_id_type=pl.DeviceIdType.MESH)
    copy.start()
    copy.wait()


class Front:
    def __init__(self, layer, sliding, refs):
        self.layer, self.sliding = layer, sliding
        (self.gain, self.cos, self.sin, self.wq, self.wk, self.wv, self.wg, self.wu, self.wd) = refs[:9]
        (self.q_o, self.k_o, self.v_o, self.m_o, self.h_o) = refs[9:14]
        (self.wq_b, self.wk_b, self.wv_b, self.wg_b, self.wu_b, self.wd_b, self.qkv_sem, self.mlp_sem) = refs[14:]

    def qkv_copies(self):
        pairs = ((self.wq, self.wq_b), (self.wk, self.wk_b), (self.wv, self.wv_b))
        return [pltpu.make_async_copy(src.at[self.layer], dst, self.qkv_sem.at[i]) for i, (src, dst) in enumerate(pairs)]

    def tile_copies(self, j, slot):
        cols = pl.ds(pl.multiple_of(j * TILE, TILE), TILE)
        return [pltpu.make_async_copy(self.wg.at[self.layer, :, cols], self.wg_b.at[slot], self.mlp_sem.at[0, slot]),
                pltpu.make_async_copy(self.wu.at[self.layer, :, cols], self.wu_b.at[slot], self.mlp_sem.at[1, slot]),
                pltpu.make_async_copy(self.wd.at[self.layer, cols, :], self.wd_b.at[slot], self.mlp_sem.at[2, slot])]

    def prefetch(self):
        for copy in self.qkv_copies():
            copy.start()
        for j in range(DEPTH):
            for copy in self.tile_copies(j, j):
                copy.start()

    def rotate(self, x):
        if not self.sliding:
            return x
        width = x.shape[1]
        first = lax.broadcasted_iota(jnp.int32, x.shape, 1) % HEAD_DIM < HEAD_DIM // 2
        swapped = jnp.where(first, pltpu.roll(x, width - HEAD_DIM // 2, 1), pltpu.roll(x, HEAD_DIM // 2, 1))
        return x * self.cos[:, :width] + swapped * self.sin[:, :width]

    def run(self, rows):
        self.h_o[...] = rows.astype(jnp.bfloat16)
        centered = rows - rows.mean(axis=-1, keepdims=True)
        variance = (centered * centered).mean(axis=-1, keepdims=True)
        scaled = centered * lax.rsqrt(variance + NORM_EPS)
        normed = (scaled * self.gain[self.layer:self.layer + 1, :].astype(jnp.float32)).astype(jnp.bfloat16)
        normed = jnp.broadcast_to(normed, (8, normed.shape[1]))
        for copy in self.qkv_copies():
            copy.wait()

        def query_step(j, carry):
            cols = pl.ds(pl.multiple_of(j * TILE, TILE), TILE)
            query = jnp.dot(normed, self.wq_b[:, cols], preferred_element_type=jnp.float32)
            self.q_o[:, cols] = self.rotate(query)[:1].astype(jnp.bfloat16)
            return carry

        lax.fori_loop(0, self.wq_b.shape[1] // TILE, query_step, 0)
        self.k_o[...] = self.rotate(jnp.dot(normed, self.wk_b[...], preferred_element_type=jnp.float32))[:1].astype(jnp.bfloat16)
        self.v_o[...] = jnp.dot(normed, self.wv_b[...], preferred_element_type=jnp.float32)[:1].astype(jnp.bfloat16)
        n_tiles = self.wg.shape[2] // TILE

        def tile_step(j, total):
            slot = lax.rem(j, DEPTH)
            for copy in self.tile_copies(j, slot):
                copy.wait()
            gate = jnp.dot(normed, self.wg_b[slot], preferred_element_type=jnp.float32)
            up = jnp.dot(normed, self.wu_b[slot], preferred_element_type=jnp.float32)
            act = (jax.nn.silu(gate) * up).astype(jnp.bfloat16)
            total = total + jnp.dot(act, self.wd_b[slot], preferred_element_type=jnp.float32)

            @pl.when(j + DEPTH < n_tiles)
            def _():
                for copy in self.tile_copies(j + DEPTH, slot):
                    copy.start()

            return total

        total = lax.fori_loop(0, n_tiles, tile_step, jnp.zeros((8, self.m_o.shape[1]), jnp.float32))
        self.m_o[...] = total[:1]


def front_shapes(dim, weights):
    q_width, kv_width = weights[0].shape[2], weights[1].shape[2]
    out = [jax.ShapeDtypeStruct((1, q_width), jnp.bfloat16), jax.ShapeDtypeStruct((1, kv_width), jnp.bfloat16),
           jax.ShapeDtypeStruct((1, kv_width), jnp.bfloat16), jax.ShapeDtypeStruct((1, dim), jnp.float32),
           jax.ShapeDtypeStruct((1, dim), jnp.bfloat16)]
    scratch = [pltpu.VMEM((dim, q_width), jnp.bfloat16), pltpu.VMEM((dim, kv_width), jnp.bfloat16),
               pltpu.VMEM((dim, kv_width), jnp.bfloat16), pltpu.VMEM((DEPTH, dim, TILE), jnp.bfloat16),
               pltpu.VMEM((DEPTH, dim, TILE), jnp.bfloat16), pltpu.VMEM((DEPTH, TILE, dim), jnp.bfloat16),
               pltpu.SemaphoreType.DMA((3,)), pltpu.SemaphoreType.DMA((3, DEPTH))]
    return out, scratch


def front_kernel(h_ref, *refs):
    part = Front(0, True, refs)
    part.prefetch()
    part.run(h_ref[...].astype(jnp.float32))


def front(h, gain, cos, sin, weights):
    out, scratch = front_shapes(h.shape[1], weights)
    return pl.pallas_call(
        front_kernel,
        out_shape=out,
        in_specs=[VMEM] * 4 + [ANY] * 6,
        out_specs=[VMEM] * 5,
        scratch_shapes=scratch,
        compiler_params=params(),
        cost_estimate=pl.CostEstimate(flops=6 * 10**9, bytes_accessed=40 * 10**6, transcendentals=0),
        name="front",
    )(h, gain, cos, sin, *weights)


def final_kernel(h_ref, part_ref, out_ref, other_ref, sems):
    greet_peer()
    swap_partials(part_ref, other_ref, sems)
    out_ref[...] = (h_ref[...].astype(jnp.float32) + (part_ref[...] + other_ref[...])).astype(jnp.bfloat16)


def final(h, part):
    return pl.pallas_call(
        final_kernel,
        out_shape=jax.ShapeDtypeStruct(h.shape, jnp.bfloat16),
        in_specs=[VMEM, VMEM], out_specs=VMEM,
        scratch_shapes=[pltpu.VMEM(part.shape, jnp.float32), pltpu.SemaphoreType.DMA((2,))],
        compiler_params=params(4, collective_id=1, has_side_effects=True),
        name="final",
    )(h, part)


def as_column(row, base):
    wide = jnp.broadcast_to(row[:, base:base + HEAD_DIM].astype(jnp.float32), (HEAD_DIM, HEAD_DIM))
    eye = (lax.broadcasted_iota(jnp.int32, wide.shape, 0) == lax.broadcasted_iota(jnp.int32, wide.shape, 1))
    return jnp.sum(jnp.where(eye, wide, 0.0), axis=1, keepdims=True).astype(jnp.bfloat16)


def spread_mask(group):
    shape = (group, group * HEAD_DIM)
    return lax.broadcasted_iota(jnp.int32, shape, 1) // HEAD_DIM == lax.broadcasted_iota(jnp.int32, shape, 0)


def attend(q_ref, k_buf, v_buf, last, wo_b, wo_copy, mlp_ref, part_o):
    kv_local = k_buf.shape[0]
    width = q_ref.shape[1] // kv_local
    spread = spread_mask(width // HEAD_DIM)
    fold = (lax.broadcasted_iota(jnp.int32, (HEAD_DIM, width), 1) % HEAD_DIM
            == lax.broadcasted_iota(jnp.int32, (HEAD_DIM, width), 0)).astype(jnp.bfloat16)
    part_o[...] = mlp_ref[...]

    def step(head, carry):
        lanes = pl.ds(pl.multiple_of(head * width, width), width)
        q_row = q_ref[:, lanes].astype(jnp.float32)
        q_wide = jnp.where(spread, jnp.broadcast_to(q_row, spread.shape), 0.0).astype(jnp.bfloat16)
        q = lax.dot_general(q_wide, fold, (((1,), (1,)), ((), ())), preferred_element_type=jnp.float32)
        scores = jnp.dot(q.astype(jnp.bfloat16), k_buf[head], preferred_element_type=jnp.float32) * HEAD_DIM ** -0.5
        if last is not None:
            valid = lax.broadcasted_iota(jnp.int32, scores.shape, 1) <= last
            scores = jnp.where(valid, scores, -1e30)
        top = jnp.max(scores, axis=1, keepdims=True)
        expd = jnp.exp(scores - top)
        weights = (expd / jnp.sum(expd, axis=1, keepdims=True)).astype(jnp.bfloat16)
        mixed = lax.dot_general(weights, v_buf[head], (((1,), (1,)), ((), ())), preferred_element_type=jnp.float32)
        wide = jnp.dot(mixed.astype(jnp.bfloat16), fold, preferred_element_type=jnp.float32)
        row = jnp.sum(jnp.where(spread, wide, 0.0), axis=0, keepdims=True).astype(jnp.bfloat16)

        @pl.when(head == 0)
        def _():
            wo_copy.wait()

        row = jnp.broadcast_to(row, (8, width))
        part_o[...] += jnp.dot(row, wo_b[lanes, :], preferred_element_type=jnp.float32)[:1]
        return carry

    lax.fori_loop(0, kv_local, step, 0)


def layer_kernel(layer, sliding_next, *refs):
    (lengths, q_ref, knew_ref, vnew_ref, mlp_ref, h_ref, k_ref, v_ref, near_ref, mine_ref, other_ref, wo) = refs[:12]
    ins, refs = refs[12:21], refs[21:]
    outs, (wk_o, wv_o), scratch = refs[:5], refs[5:7], refs[7:]
    (k_buf, v_buf, k_far, v_far, wo_b, near_sem, far_sem, wo_sem, out_sem, part_b, other_b, rdma_sem) = scratch[:12]
    front_part = Front(layer + 1, sliding_next, (*ins, *outs, *scratch[12:]))
    greet_peer()
    row, core, chip = place()
    turn = lengths[row] - WINDOW
    start, _ = far_chunks(lengths[row], chip == 0)
    _, count0 = far_chunks(lengths[2 * chip], chip == 0)
    shift = jnp.where(core == 0, 0, count0) - start
    n_far = k_far.shape[0]
    own = pl.ds(pl.multiple_of(core * SHARD, SHARD), SHARD)
    peer = pl.ds(pl.multiple_of((1 - core) * SHARD, SHARD), SHARD)
    loads = [pltpu.make_async_copy(k_ref.at[layer, row], k_buf.at[:, :, own], near_sem.at[0]),
             pltpu.make_async_copy(v_ref.at[layer, row], v_buf.at[:, :, own], near_sem.at[1]),
             pltpu.make_async_copy(near_ref.at[0, 0], k_buf.at[:, :, peer], near_sem.at[2]),
             pltpu.make_async_copy(near_ref.at[0, 1], v_buf.at[:, :, peer], near_sem.at[3])]

    @pl.when(core == 0)
    def _():
        pltpu.make_async_copy(mine_ref, k_far, far_sem.at[0]).start()
        pltpu.make_async_copy(other_ref, v_far, far_sem.at[1]).start()

    @pl.when(core == 1)
    def _():
        pltpu.make_async_copy(other_ref, k_far, far_sem.at[0]).start()
        pltpu.make_async_copy(mine_ref, v_far, far_sem.at[1]).start()

    for copy in loads:
        copy.start()
    wo_copy = pltpu.make_async_copy(wo.at[layer], wo_b, wo_sem)
    wo_copy.start()
    k_new = [as_column(knew_ref[...], head * HEAD_DIM) for head in range(2)]
    v_new = [as_column(vnew_ref[...], head * HEAD_DIM) for head in range(2)]
    for copy in loads:
        copy.wait()
    pltpu.make_async_copy(mine_ref, k_far, far_sem.at[0]).wait()
    pltpu.make_async_copy(mine_ref, v_far, far_sem.at[1]).wait()
    front_part.prefetch()

    def step(c, carry):
        lanes = pl.ds(pl.multiple_of(c * CHUNK, CHUNK), CHUNK)
        piece = jnp.clip(c + shift, 0, n_far - 1)
        slots = c * CHUNK + lax.broadcasted_iota(jnp.int32, (HEAD_DIM, CHUNK), 1)
        from_far = jnp.where(chip == 0, turn - slots, slots - turn) > 0
        is_new = slots == turn
        for head in range(2):
            for buf, far, new in ((k_buf, k_far, k_new), (v_buf, v_far, v_new)):
                near = buf[head, :, lanes]
                mixed = jnp.where(from_far, far[piece, head], near)
                buf[head, :, lanes] = jnp.where(is_new, jnp.broadcast_to(new[head], near.shape), mixed)
        return carry

    lax.fori_loop(0, WINDOW // CHUNK, step, 0)
    stores = [pltpu.make_async_copy(k_buf, wk_o, out_sem.at[0]),
              pltpu.make_async_copy(v_buf, wv_o, out_sem.at[1])]
    for copy in stores:
        copy.start()
    attend(q_ref, k_buf, v_buf, None, wo_b, wo_copy, mlp_ref, part_b)
    swap_partials(part_b, other_b, rdma_sem)
    rows = h_ref[...].astype(jnp.float32) + (part_b[...] + other_b[...])
    front_part.run(rows.astype(jnp.bfloat16).astype(jnp.float32))
    for copy in stores:
        copy.wait()


def sliding_layer(layer, sliding_next, lengths, state, k_t, v_t, near, mine, other, wo, gain, cos, sin, weights):
    dim = state[-1].shape[1]
    args = [lengths, *state, k_t, v_t, near, mine, other, wo, gain, cos, sin, *weights]
    specs = [SMEM] + [VMEM] * 5 + [ANY] * 3 + [EITHER] * 2 + [ANY] + [VMEM] * 3 + [ANY] * 6
    buf = pltpu.VMEM((2, HEAD_DIM, WINDOW), jnp.bfloat16)
    far = pltpu.VMEM(mine.shape, jnp.bfloat16)
    out = jax.ShapeDtypeStruct((2, HEAD_DIM, WINDOW), jnp.bfloat16)
    front_out, front_scratch = front_shapes(dim, weights)
    result = pl.pallas_call(
        functools.partial(layer_kernel, layer, sliding_next),
        out_shape=front_out + [out, out],
        in_specs=specs, out_specs=[VMEM] * 5 + [ANY, ANY],
        scratch_shapes=[buf, buf, far, far, pltpu.VMEM(wo.shape[1:], jnp.bfloat16),
                        pltpu.SemaphoreType.DMA((4,)), pltpu.SemaphoreType.DMA((2,)),
                        pltpu.SemaphoreType.DMA, pltpu.SemaphoreType.DMA((2,)),
                        pltpu.VMEM((1, dim), jnp.float32), pltpu.VMEM((1, dim), jnp.float32),
                        pltpu.SemaphoreType.DMA((2,))] + front_scratch,
        compiler_params=params(collective_id=5 + 6 * SIZES.index(mine.shape[0]) + layer, has_side_effects=True),
        cost_estimate=pl.CostEstimate(flops=8 * 10**9, bytes_accessed=52 * 2**20, transcendentals=0),
    )(*args)
    return result[:5], result[5:]


def emit_kernel(layer, wk_ref, wv_ref, *refs):
    wk_o, wv_o, buf, in_sem, out_sem = refs[-5:]
    arrivals = [pltpu.make_async_copy(ref, buf.at[i], in_sem.at[i]) for i, ref in enumerate((wk_ref, wv_ref))]
    departures = [pltpu.make_async_copy(buf.at[i], ref.at[layer], out_sem.at[i]) for i, ref in enumerate((wk_o, wv_o))]
    for copy in arrivals:
        copy.start()
    for arrival, departure in zip(arrivals, departures):
        arrival.wait()
        departure.start()
    for copy in departures:
        copy.wait()


def emit(layer, windows, outs):
    out = jax.ShapeDtypeStruct((3,) + windows[0].shape, jnp.bfloat16)
    return pl.pallas_call(
        functools.partial(emit_kernel, layer),
        out_shape=[out, out],
        in_specs=[ANY] * (2 + len(outs)), out_specs=[ANY] * 2,
        scratch_shapes=[pltpu.VMEM((2,) + windows[0].shape, jnp.bfloat16), pltpu.SemaphoreType.DMA((2,)),
                        pltpu.SemaphoreType.DMA((2,))],
        input_output_aliases={2: 0, 3: 1} if outs else {},
        compiler_params=params(),
        cost_estimate=pl.CostEstimate(flops=10**9, bytes_accessed=4 * 2**20, transcendentals=0),
    )(*windows, *outs)


def global_kernel(layer, lengths, q_ref, knew_ref, vnew_ref, mlp_ref, k_ref, v_ref, near_ref, *refs):
    pieces = refs[:4]
    (wo, wk_ref, wv_ref, _, _, part_o, gk_o, gv_o, wk_o, wv_o, k_buf, v_buf, wo_b, w_buf, load_sem, wo_sem, out_sem,
     pass_in, pass_out) = refs[4:]
    arrivals = [pltpu.make_async_copy(ref, w_buf.at[i], pass_in.at[i]) for i, ref in enumerate((wk_ref, wv_ref))]
    departures = [pltpu.make_async_copy(w_buf.at[i], ref.at[layer - 1], pass_out.at[i]) for i, ref in enumerate((wk_o, wv_o))]
    row, core, chip = place()
    last = lengths[row]
    across = row + 2 - 4 * chip
    sources = (row + 1 - 2 * core, across, across + 1 - 2 * core)
    lanes = [pl.ds(pl.multiple_of(shard * SHARD, SHARD), SHARD) for shard in (row,) + sources]
    parts = [k_ref.at[layer, row], v_ref.at[layer, row], near_ref.at[1, 0], near_ref.at[1, 1], *pieces]
    loads = [pltpu.make_async_copy(ref, (k_buf, v_buf)[i % 2].at[:, :, lanes[i // 2]], load_sem.at[i])
             for i, ref in enumerate(parts)]
    for copy in loads:
        copy.start()
    wo_copy = pltpu.make_async_copy(wo.at[layer], wo_b, wo_sem)
    wo_copy.start()
    for copy in arrivals:
        copy.start()
    k_new = [as_column(knew_ref[...], head * HEAD_DIM) for head in range(2)]
    v_new = [as_column(vnew_ref[...], head * HEAD_DIM) for head in range(2)]
    for copy in loads:
        copy.wait()

    def step(c, carry):
        lanes = pl.ds(pl.multiple_of(c * CHUNK, CHUNK), CHUNK)
        slots = c * CHUNK + lax.broadcasted_iota(jnp.int32, (HEAD_DIM, CHUNK), 1)
        for head in range(2):
            for buf, new in ((k_buf, k_new), (v_buf, v_new)):
                near = buf[head, :, lanes]
                kept = jnp.where(slots < last, near, jnp.zeros_like(near))
                buf[head, :, lanes] = jnp.where(slots == last, jnp.broadcast_to(new[head], near.shape), kept)
        return carry

    lax.fori_loop(last // CHUNK, 2 * WINDOW // CHUNK, step, 0)
    stores = [pltpu.make_async_copy(k_buf, gk_o, out_sem.at[0]), pltpu.make_async_copy(v_buf, gv_o, out_sem.at[1])]
    for copy in stores:
        copy.start()
    for arrival, departure in zip(arrivals, departures):
        arrival.wait()
        departure.start()
    attend(q_ref, k_buf, v_buf, last, wo_b, wo_copy, mlp_ref, part_o)
    for copy in stores + departures:
        copy.wait()


def global_layer(layer, lengths, q, k_new, v_new, mlp, k_t, v_t, pieces, wo, windows, outs):
    buf = pltpu.VMEM((2, HEAD_DIM, 4 * SHARD), jnp.bfloat16)
    out = jax.ShapeDtypeStruct((2, HEAD_DIM, 4 * SHARD), jnp.bfloat16)
    window = jax.ShapeDtypeStruct(outs[0].shape, jnp.bfloat16)
    return pl.pallas_call(
        functools.partial(global_kernel, layer),
        out_shape=[jax.ShapeDtypeStruct(mlp.shape, jnp.float32), out, out, window, window],
        in_specs=[SMEM] + [VMEM] * 4 + [ANY] * 12, out_specs=[VMEM] + [ANY] * 4,
        scratch_shapes=[buf, buf, pltpu.VMEM(wo.shape[1:], jnp.bfloat16), pltpu.VMEM((2,) + windows[0].shape, jnp.bfloat16),
                        pltpu.SemaphoreType.DMA((8,)), pltpu.SemaphoreType.DMA, pltpu.SemaphoreType.DMA((2,)),
                        pltpu.SemaphoreType.DMA((2,)), pltpu.SemaphoreType.DMA((2,))],
        input_output_aliases={15: 3, 16: 4},
        compiler_params=params(),
        cost_estimate=pl.CostEstimate(flops=3 * 10**9, bytes_accessed=26 * 2**20, transcendentals=0),
        name="global",
    )(lengths, q, k_new, v_new, mlp, k_t, v_t, *pieces, wo, *windows, *outs)


def run_layers(n_chunks, same_k, k_t, v_t, lengths, residual, ln_gain, weights, w_out):
    last = w_out.shape[0] - 1
    same_k = lax.ppermute(same_k, "sp", CROSS)
    streams = []
    for layer in range(last):
        traded = ((layer, True),) if layer < last - 1 else ((layer, True), (last, False))
        far, near = swap(traded, k_t, v_t, 2 + layer)
        packed = pack(layer, n_chunks, lengths, k_t, v_t, far)
        mine = lax.ppermute(packed, "sp", CROSS)
        other = lax.ppermute(mine, "sp", PARTNER)
        streams.append((near, mine, other))
    same_v, cross_k, cross_v = payload(last, (("same", 1), ("cross", 0), ("cross", 1)), k_t, v_t)
    same_v = lax.ppermute(same_v, "sp", CROSS)
    cross_k = lax.ppermute(cross_k, "sp", CROSS_SWAP)
    cross_v = lax.ppermute(cross_v, "sp", CROSS_SWAP)

    my_length = lengths[lax.axis_index("sp")]
    half_dim = HEAD_DIM // 2
    inv_freq = 1.0 / (ROPE_BASE ** (jnp.arange(half_dim, dtype=jnp.float32) * 2.0 / HEAD_DIM))
    angles = my_length.astype(jnp.float32) * inv_freq
    cosine, sine = jnp.cos(angles), jnp.sin(angles)
    cos = jnp.tile(jnp.concatenate([cosine, cosine]), TILE // HEAD_DIM)[None]
    sin = jnp.tile(jnp.concatenate([-sine, sine]), TILE // HEAD_DIM)[None]

    state = front(residual, ln_gain, cos, sin, weights)
    outs = ()
    for layer in range(last):
        state, windows = sliding_layer(layer, layer + 1 < last, lengths, state, k_t, v_t, *streams[layer], w_out,
                                       ln_gain, cos, sin, weights)
        if layer + 1 < last:
            outs = emit(layer, windows, outs)
    return state, (near, same_k, same_v, cross_k, cross_v), windows, outs


def decode(k_t, v_t, lengths, hidden, ln_gain, w_query, w_key, w_value, w_out, w_gate, w_up, w_down):
    weights = (w_query, w_key, w_value, w_gate, w_up, w_down)

    counts = far_chunks(lengths, jnp.arange(4) < 2)[1]
    needed = jnp.maximum(counts[0] + counts[1], counts[2] + counts[3])
    choice = sum((needed > size).astype(jnp.int32) for size in SIZES[:-1])

    def branch(i):
        def run(args):
            return run_layers(SIZES[i], *args)

        return run

    (same_k,) = payload(w_out.shape[0] - 1, (("same", 0),), k_t, v_t)
    args = (same_k, k_t, v_t, lengths, hidden, ln_gain, weights, w_out)
    state, pieces, windows, outs = lax.switch(choice, [branch(i) for i in range(len(SIZES))], args)
    *inputs, residual = state
    part, *caches = global_layer(w_out.shape[0] - 1, lengths, *inputs, k_t, v_t, pieces, w_out, windows, outs)
    global_k, global_v, window_k, window_v = caches
    return final(residual, part), window_k, window_v, global_k, global_v


SIZES = (34, 50, 64)


def solution(mesh):
    cache_spec = P(None, "dp", "tp", "sp", None)
    row_spec = P(("dp", "sp"), None)
    col_spec = P(None, None, "tp")
    inner_spec = P(None, "tp", None)
    window_spec = P(None, ("dp", "sp"), "tp", None, None)
    global_spec = P(("dp", "sp"), "tp", None, None)
    in_specs = (cache_spec, cache_spec, P("dp"), row_spec, P(None, None), col_spec, col_spec, col_spec, inner_spec, col_spec, col_spec, inner_spec)
    out_specs = (row_spec, window_spec, window_spec, global_spec, global_spec)

    def device_step(k_cache, v_cache, *rest):
        k_t, v_t = jnp.swapaxes(k_cache, 3, 4), jnp.swapaxes(v_cache, 3, 4)
        h, wk, wv, gk, gv = decode(k_t, v_t, *rest)
        turn = lambda x: jnp.swapaxes(x, -1, -2)
        return h, turn(wk)[:, None], turn(wv)[:, None], turn(gk)[None], turn(gv)[None]

    return jax.shard_map(device_step, mesh=mesh, in_specs=in_specs, out_specs=out_specs, check_vma=False)
```

time: 174 us -> 175 us (level)
  waiting for transfers between devices: 28.2 us -> 31.2 us
  Pallas kernels: 129 us -> 127 us
    ppermute x3, waiting for transfers between devices: 28.2 us -> 31.2 us  [run_layers(): mine = lax.ppermute(packed, 'sp', CROSS)]
    pallas_call x7 -> x6, Pallas kernels: 83.4 us -> 81.1 us  [the longest x3 59.5 us: sliding_layer(): pl.pallas_call(functools.partial(layer_kernel, layer, sliding_next), out_...]
    pallas_call x1, Pallas kernels: 5.47 us -> 3.7 us  [final(): pl.pallas_call(final_kernel, out_shape=jax.ShapeDtypeStruct(h.shape, jnp....]
  transfers between devices with their start and end apart: 10 -> 10, of which waited for: 3 -> 3; matrix products, arithmetic and copies ran while one was open for 1% -> 1% of each run, Pallas kernels for 62% -> 59%
where the time goes in v1:
time: 175 us; the launch traced here: 174 us
  Pallas kernels  127 us (73%)
  waiting for transfers between devices  31.2 us (18%)
  starting transfers between devices  7.12 us (4%)
  local copies, waits for them, and re-layouts  3.7 us (2%)
  between operations  3.35 us (2%)
    pallas_call x3, Pallas kernels, sliding_layer(): pl.pallas_call(functools.partial(layer_kernel, layer, sliding_next), out_...  59.5 us
    ppermute x3, waiting for transfers between devices, run_layers(): mine = lax.ppermute(packed, 'sp', CROSS)  31.2 us
    pallas_call x1, Pallas kernels, front(): pl.pallas_call(front_kernel, out_shape=out, in_specs=[VMEM] * 4 + [ANY] *...  16.2 us
    pallas_call x3, Pallas kernels, swap(): pl.pallas_call(functools.partial(swap_kernel, layers), out_shape=[block,...  15.7 us
    pallas_call x3, Pallas kernels, pack(): pl.pallas_call(functools.partial(pack_kernel, layer, n_chunks), out_shape...  12.7 us
    pallas_call x1, Pallas kernels, global_layer(): pl.pallas_call(functools.partial(global_kernel, layer), out_shape=[jax.Sh...  8.74 us
    pallas_call x2, Pallas kernels, emit(): pl.pallas_call(functools.partial(emit_kernel, layer), out_shape=[out, out...  5.4 us
    pallas_call x2, Pallas kernels, payload(): pl.pallas_call(functools.partial(payload_kernel, layer, picks), out_shape...  4.53 us
  transfers between devices with their start and end apart: 10, of which 3 were waited for; matrix products, arithmetic and copies ran while one was open for 1% of the time, Pallas kernels for 59%

profile of v1, /device:TPU:0, one launch (start us, length us, event | category | flops | bytes accessed | tf_op | source)
XLA Modules:
  0.0 173.9 jit_solution(7466790841485837975)
XLA Ops:
  0.6 0.7 compare_select_fusion
  1.3 0.6 fusion.9
  4.5 2.0 %payload.7 = bf16[2,64,2048]{2,1,0:T(8,128)(2,1)} custom-call(bf16[4,4,2,64,2048]{4,3,2,1,0:T(8,128)(2,1)} %bitcast.22, bf16[4,4,2,64,2048]{4,3,2,1,0:T(8,128)(2,1)} %bitcast.27), custom_call_target="tpu_custom_call" | custom-call | flops 1000000000 | bytes 1048576 | tf_op jit(solution)/shard_map/payload/pallas_call | solution.py:151
  6.6 153.7 %conditional.1 = (bf16[1,1024]{1,0:T(2,128)(2,1)S(1)}, bf16[1,128]{1,0:T(2,128)(2,1)S(1)}, bf16[1,128]{1,0:T(2,128)(2,1)}, f32[1,2048]{1,0:T(1,128)S(1)}, bf16[1...) conditional(s32[]{:T(128)} %bitcast.3, (s32[4]{0:T(128)S(1)}, ...), branch_computations={%region_0.1_spmd, %region_1.2_spmd, %region_2.3_spmd} | conditional | flops 39000002560 | bytes 321813440 | solution.py:576
  6.6 5.0 %swap.9 = (bf16[1,2,2,64,2048]{4,3,2,1,0:T(8,128)(2,1)}, bf16[1,2,2,64,2048]{4,3,2,1,0:T(8,128)(2,1)}) custom-call(bf16[4,4,2,64,2048]{4,3,2,1,0:T(8,128)(2,1)} %get-tuple-element.92.k_ref.refs_6_, bf16[4,4,2,64,2048]{4,3,2,1,0:T(8,128)(2,1)} %get-tuple-element.93.v_ref.refs_7_), custom_call_target="tpu_custom_call" | custom-call | flops 1000000000 | bytes 4194304 | tf_op jit(solution)/shard_map/cond/branch_0_fun/swap/pallas_call | solution.py:83
  11.7 4.0 %branch_0_fun.8 = bf16[34,2,64,128]{3,2,1,0:T(8,128)(2,1)} custom-call(s32[4]{0:T(128)S(1)} %get-tuple-element.78.lengths.refs_0_, bf16[4,4,2,64,2048]{4,3,2,1,0:T(8,128)(2,1)} %get-tuple-element.92.k_ref.refs_6_, bf16[4,4,2,64,2048]{4,3,2,1,0:T(8,128)(2,1)} %get-tuple-element.93.v_ref.refs_7_, bf16[1,2,2,64,2048]{4,3,2,1,0:T(8,128)(2,1)} %get-tuple-element.95.recv_ref), custom_call_target="tpu_custom_call" | custom-call | flops 1000000000 | bytes 4194304 | tf_op jit(solution)/shard_map/cond/branch_0_fun/pallas_call | solution.py:127
  15.7 1.9 %collective-permute-start = (bf16[34,2,64,128]{3,2,1,0:T(8,128)(2,1)}, bf16[34,2,64,128]{3,2,1,0:T(8,128)(2,1)}, u32[]{:S(2)}, u32[]{:S(2)}) collective-permute-start(bf16[34,2,64,128]{3,2,1,0:T(8,128)(2,1)} %branch_0_fun.8), channel_id=1, source_target_pairs={{0,2},{2,0},{1,3},{3,1},{4,6},{6,4},{5,7},{7,5}} | collective-permute-start | bytes 3342344 | tf_op jit(solution)/shard_map/cond/branch_0_fun/ppermute | solution.py:535
  17.6 4.6 %swap.10 = (bf16[1,2,2,64,2048]{4,3,2,1,0:T(8,128)(2,1)}, bf16[1,2,2,64,2048]{4,3,2,1,0:T(8,128)(2,1)}) custom-call(bf16[4,4,2,64,2048]{4,3,2,1,0:T(8,128)(2,1)} %get-tuple-element.92.k_ref.refs_6_, bf16[4,4,2,64,2048]{4,3,2,1,0:T(8,128)(2,1)} %get-tuple-element.93.v_ref.refs_7_), custom_call_target="tpu_custom_call" | custom-call | flops 1000000000 | bytes 4194304 | tf_op jit(solution)/shard_map/cond/branch_0_fun/swap/pallas_call | solution.py:83
  22.1 4.0 %branch_0_fun.10 = bf16[34,2,64,128]{3,2,1,0:T(8,128)(2,1)} custom-call(s32[4]{0:T(128)S(1)} %get-tuple-element.78.lengths.refs_0_, bf16[4,4,2,64,2048]{4,3,2,1,0:T(8,128)(2,1)} %get-tuple-element.92.k_ref.refs_6_, bf16[4,4,2,64,2048]{4,3,2,1,0:T(8,128)(2,1)} %get-tuple-element.93.v_ref.refs_7_, bf16[1,2,2,64,2048]{4,3,2,1,0:T(8,128)(2,1)} %get-tuple-element.103.recv_ref), custom_call_target="tpu_custom_call" | custom-call | flops 1000000000 | bytes 4194304 | tf_op jit(solution)/shard_map/cond/branch_0_fun/pallas_call | solution.py:127
  26.2 6.1 %swap.11 = (bf16[2,2,2,64,2048]{4,3,2,1,0:T(8,128)(2,1)}, bf16[2,2,2,64,2048]{4,3,2,1,0:T(8,128)(2,1)}) custom-call(bf16[4,4,2,64,2048]{4,3,2,1,0:T(8,128)(2,1)} %get-tuple-element.92.k_ref.refs_6_, bf16[4,4,2,64,2048]{4,3,2,1,0:T(8,128)(2,1)} %get-tuple-element.93.v_ref.refs_7_), custom_call_target="tpu_custom_call" | custom-call | flops 1000000000 | bytes 4194304 | tf_op jit(solution)/shard_map/cond/branch_0_fun/swap/pallas_call | solution.py:83
  32.3 4.7 %branch_0_fun.12 = bf16[34,2,64,128]{3,2,1,0:T(8,128)(2,1)} custom-call(s32[4]{0:T(128)S(1)} %get-tuple-element.78.lengths.refs_0_, bf16[4,4,2,64,2048]{4,3,2,1,0:T(8,128)(2,1)} %get-tuple-element.92.k_ref.refs_6_, bf16[4,4,2,64,2048]{4,3,2,1,0:T(8,128)(2,1)} %get-tuple-element.93.v_ref.refs_7_, bf16[2,2,2,64,2048]{4,3,2,1,0:T(8,128)(2,1)} %get-tuple-element.110.recv_ref), custom_call_target="tpu_custom_call" | custom-call | flops 1000000000 | bytes 4194304 | tf_op jit(solution)/shard_map/cond/branch_0_fun/pallas_call | solution.py:127
  37.0 0.4 collective-permute-start.4
  37.4 6.0 %collective-permute-done.refs_9_ = bf16[34,2,64,128]{3,2,1,0:T(8,128)(2,1)} collective-permute-done((bf16[34,2,64,128]{3,2,1,0:T(8,128)(2,1)}, bf16[34,2,64,128]{3,2,1,0:T(8,128)(2,1)}, u32[]{:S(2)}, u32[]{:S(2)}) %collective-permute-start) | collective-permute-done | bytes 1114144 | tf_op jit(solution)/shard_map/cond/branch_0_fun/ppermute | solution.py:535
  43.5 1.9 %collective-permute-start.6 = (bf16[2,64,2048]{2,1,0:T(8,128)(2,1)}, bf16[2,64,2048]{2,1,0:T(8,128)(2,1)}, u32[]{:S(2)}, u32[]{:S(2)}) collective-permute-start(bf16[2,64,2048]{2,1,0:T(8,128)(2,1)} %get-tuple-element.116), channel_id=1, source_target_pairs={{0,2},{2,0},{1,3},{3,1},{4,6},{6,4},{5,7},{7,5}} | collective-permute-start | bytes 1572872 | tf_op jit(solution)/shard_map/cond/branch_0_fun/ppermute | solution.py:529
  45.3 2.5 %payload.4 = (bf16[2,64,2048]{2,1,0:T(8,128)(2,1)}, bf16[2,64,2048]{2,1,0:T(8,128)(2,1)}, bf16[2,64,2048]{2,1,0:T(8,128)(2,1)}) custom-call(bf16[4,4,2,64,2048]{4,3,2,1,0:T(8,128)(2,1)} %get-tuple-element.92.k_ref.refs_6_, bf16[4,4,2,64,2048]{4,3,2,1,0:T(8,128)(2,1)} %get-tuple-element.93.v_ref.refs_7_), custom_call_target="tpu_custom_call" | custom-call | flops 1000000000 | bytes 3145728 | tf_op jit(solution)/shard_map/cond/branch_0_fun/payload/pallas_call | solution.py:151
  48.0 0.6 dynamic_slice.6
  49.7 17.6 %collective-permute-done.2.refs_9_ = bf16[34,2,64,128]{3,2,1,0:T(8,128)(2,1)} collective-permute-done((bf16[34,2,64,128]{3,2,1,0:T(8,128)(2,1)}, bf16[34,2,64,128]{3,2,1,0:T(8,128)(2,1)}, u32[]{:S(2)}, u32[]{:S(2)}) %collective-permute-start.2) | collective-permute-done | bytes 1114144 | tf_op jit(solution)/shard_map/cond/branch_0_fun/ppermute | solution.py:535
  67.3 16.2 %front.3 = (bf16[1,1024]{1,0:T(2,128)(2,1)S(1)}, bf16[1,128]{1,0:T(2,128)(2,1)S(1)}, bf16[1,128]{1,0:T(2,128)(2,1)S(1)}, f32[1,2048]{1,0:T(1,128)S(1)}, bf16[1,2048]{1,0:T(2,128)(2,1)S(1)}) custom-call(bf16[1,2048]{1,0:T(2,128)(2,1)S(1)} %get-tuple-element.79.h_ref, bf16[4,2048]{1,0:T(4,128)(2,1)S(1)} %get-tuple-element.80.refs_0_.refs_12_, ...), custom_call_target="tpu_custom_call" | custom-call | flops 6000000000 | bytes 40000000 | tf_op jit(solution)/shard_map/cond/branch_0_fun/front/pallas_call | solution.py:269
  83.6 7.5 %collective-permute-done.4.refs_9_ = bf16[34,2,64,128]{3,2,1,0:T(8,128)(2,1)S(1)} collective-permute-done((bf16[34,2,64,128]{3,2,1,0:T(8,128)(2,1)}, bf16[34,2,64,128]{3,2,1,0:T(8,128)(2,1)S(1)}, u32[]{:S(2)}, u32[]{:S(2)}) %collective-permute-start.4) | collective-permute-done | bytes 1114144 | tf_op jit(solution)/shard_map/cond/branch_0_fun/ppermute | solution.py:535
  91.1 2.0 %collective-permute-start.5 = (bf16[34,2,64,128]{3,2,1,0:T(8,128)(2,1)S(1)}, bf16[34,2,64,128]{3,2,1,0:T(8,128)(2,1)S(1)}, u32[]{:S(2)}, u32[]{:S(2)}) collective-permute-start(bf16[34,2,64,128]{3,2,1,0:T(8,128)(2,1)S(1)} %collective-permute-done.4.refs_9_), channel_id=1, source_target_pairs={{0,1},{1,0},{2,3},{3,2},{4,5},{5,4},{6,7},{7,6}} | collective-permute-start | bytes 3342344 | tf_op jit(solution)/shard_map/cond/branch_0_fun/ppermute | solution.py:536
  93.1 20.1 %branch_0_fun.9 = (bf16[1,1024]{1,0:T(2,128)(2,1)S(1)}, bf16[1,128]{1,0:T(2,128)(2,1)S(1)}, bf16[1,128]{1,0:T(2,128)(2,1)S(1)}, f32[1,2048]{1,0:T(1,128)S(1)}, b...) custom-call(s32[4]{0:T(128)S(1)} %get-tuple-element.78.lengths.refs_0_, ...), custom_call_target="tpu_custom_call" | custom-call | flops 8000000000 | bytes 54525952 | tf_op jit(solution)/shard_map/cond/branch_0_fun/pallas_call | solution.py:420
  113.2 2.7 %branch_0_fun.14 = (bf16[3,2,64,4096]{3,2,1,0:T(8,128)(2,1)}, bf16[3,2,64,4096]{3,2,1,0:T(8,128)(2,1)}) custom-call(bf16[2,64,4096]{2,1,0:T(8,128)(2,1)S(1)} %get-tuple-element.124.wk_ref, bf16[2,64,4096]{2,1,0:T(8,128)(2,1)} %get-tuple-element.125.wv_ref), custom_call_target="tpu_custom_call" | custom-call | flops 1000000000 | bytes 4194304 | tf_op jit(solution)/shard_map/cond/branch_0_fun/pallas_call | solution.py:450
  115.9 0.8 collective-permute-start.9
  116.7 0.2 copy-done.9
  116.9 19.1 %branch_0_fun.11 = (bf16[1,1024]{1,0:T(2,128)(2,1)S(1)}, bf16[1,128]{1,0:T(2,128)(2,1)S(1)}, bf16[1,128]{1,0:T(2,128)(2,1)S(1)}, f32[1,2048]{1,0:T(1,128)S(1)}, ...) custom-call(s32[4]{0:T(128)S(1)} %get-tuple-element.78.lengths.refs_0_, ...), custom_call_target="tpu_custom_call" | custom-call | flops 8000000000 | bytes 54525952 | tf_op jit(solution)/shard_map/cond/branch_0_fun/pallas_call | solution.py:420
  136.0 2.7 %branch_0_fun.15 = (bf16[3,2,64,4096]{3,2,1,0:T(8,128)(2,1)}, bf16[3,2,64,4096]{3,2,1,0:T(8,128)(2,1)}) custom-call(bf16[2,64,4096]{2,1,0:T(8,128)(2,1)S(1)} %get-tuple-element.122.wk_ref, bf16[2,64,4096]{2,1,0:T(8,128)(2,1)} %get-tuple-element.123.wv_ref, ...), custom_call_target="tpu_custom_call", output_to_operand_aliasing={{0}: (2, {}), {1}: (3, {})} | custom-call | flops 1000000000 | bytes 4194304 | tf_op jit(solution)/shard_map/cond/branch_0_fun/pallas_call | solution.py:450
  138.7 1.0 copy-done.8
  139.7 20.3 %branch_0_fun.13 = (bf16[1,1024]{1,0:T(2,128)(2,1)S(1)}, bf16[1,128]{1,0:T(2,128)(2,1)S(1)}, bf16[1,128]{1,0:T(2,128)(2,1)}, f32[1,2048]{1,0:T(1,128)S(1)}, bf16...) custom-call(s32[4]{0:T(128)S(1)} %get-tuple-element.78.lengths.refs_0_, ...), custom_call_target="tpu_custom_call" | custom-call | flops 8000000000 | bytes 54525952 | tf_op jit(solution)/shard_map/cond/branch_0_fun/pallas_call | solution.py:420
  160.4 0.5 copy-done.13
  160.9 8.7 %global.1 = (f32[1,2048]{1,0:T(1,128)S(1)}, bf16[2,64,8192]{2,1,0:T(8,128)(2,1)}, bf16[2,64,8192]{2,1,0:T(8,128)(2,1)}, bf16[3,2,64,4096]{3,2,1,0:T(8,128)(2,1)}, bf16[3,2,64,4096]{3,2,1,0:T(8,128)(2,1)}) custom-call(s32[4]{0:T(128)S(1)} %copy-done.10, bf16[1,1024]{1,0:T(2,128)(2,1)S(1)} %get-tuple-element.259.q_ref, ...), custom_call_target="tpu_custom_call", output_to_operand_aliasing={{3}: (15, {}), {4}: (16, {})} | custom-call | flops 3000000000 | bytes 27262976 | tf_op jit(solution)/shard_map/global/pallas_call | solution.py:513
  169.6 3.7 %final.1 = bf16[1,2048]{1,0:T(2,128)(2,1)S(1)} custom-call(bf16[1,2048]{1,0:T(2,128)(2,1)S(1)} %copy-done.12, f32[1,2048]{1,0:T(1,128)S(1)} %get-tuple-element.272.part_ref), custom_call_target="tpu_custom_call" | custom-call | tf_op jit(solution)/shard_map/final/pallas_call | solution.py:288
  173.3 0.6 copy.78
  (37 shorter events, 0.7 us)
Async XLA Ops:
  4.5 2.1 %copy-start = (bf16[4,2048,128]{2,1,0:T(8,128)(2,1)S(1)}, bf16[4,2048,128]{2,1,0:T(8,128)(2,1)}, u32[]{:S(2)}) copy-start(bf16[4,2048,128]{2,1,0:T(8,128)(2,1)} %param.21) | copy-start | bytes 6291460
  4.5 2.1 %copy-start.6 = (bf16[4,2048]{1,0:T(4,128)(2,1)S(1)}, bf16[4,2048]{1,0:T(4,128)(2,1)}, u32[]{:S(2)}) copy-start(bf16[4,2048]{1,0:T(4,128)(2,1)} %param.19) | copy-start | bytes 49156
  4.5 2.1 %copy-start.10 = (s32[4]{0:T(128)S(1)}, s32[4]{0:T(128)}, u32[]{:S(2)}) copy-start(s32[4]{0:T(128)} %lengths.1) | copy-start | bytes 52
  4.5 2.1 %copy-start.11 = (bf16[1,2048]{1,0:T(2,128)(2,1)S(1)}, bf16[1,2048]{1,0:T(2,128)(2,1)}, u32[]{:S(2)}) copy-start(bf16[1,2048]{1,0:T(2,128)(2,1)} %param.18) | copy-start | bytes 12292
  15.7 27.8 %collective-permute-start = (bf16[34,2,64,128]{3,2,1,0:T(8,128)(2,1)}, bf16[34,2,64,128]{3,2,1,0:T(8,128)(2,1)}, u32[]{:S(2)}, u32[]{:S(2)}) collective-permute-start(bf16[34,2,64,128]{3,2,1,0:T(8,128)(2,1)} %branch_0_fun.8), channel_id=1, source_target_pairs={{0,2},{2,0},{1,3},{3,1},{4,6},{6,4},{5,7},{7,5}} | collective-permute-start | bytes 3342344 | tf_op jit(solution)/shard_map/cond/branch_0_fun/ppermute | solution.py:535
  26.2 41.2 %collective-permute-start.2 = (bf16[34,2,64,128]{3,2,1,0:T(8,128)(2,1)}, bf16[34,2,64,128]{3,2,1,0:T(8,128)(2,1)}, u32[]{:S(2)}, u32[]{:S(2)}) collective-permute-start(bf16[34,2,64,128]{3,2,1,0:T(8,128)(2,1)} %branch_0_fun.10), channel_id=1, source_target_pairs={{0,2},{2,0},{1,3},{3,1},{4,6},{6,4},{5,7},{7,5}} | collective-permute-start | bytes 3342344 | tf_op jit(solution)/shard_map/cond/branch_0_fun/ppermute | solution.py:535
  37.0 54.1 %collective-permute-start.4 = (bf16[34,2,64,128]{3,2,1,0:T(8,128)(2,1)}, bf16[34,2,64,128]{3,2,1,0:T(8,128)(2,1)S(1)}, u32[]{:S(2)}, u32[]{:S(2)}) collective-permute-start(bf16[34,2,64,128]{3,2,1,0:T(8,128)(2,1)} %branch_0_fun.12), channel_id=1, source_target_pairs={{0,2},{2,0},{1,3},{3,1},{4,6},{6,4},{5,7},{7,5}} | collective-permute-start | bytes 3342344 | tf_op jit(solution)/shard_map/cond/branch_0_fun/ppermute | solution.py:535
  43.5 47.7 %collective-permute-start.1 = (bf16[34,2,64,128]{3,2,1,0:T(8,128)(2,1)}, bf16[34,2,64,128]{3,2,1,0:T(8,128)(2,1)}, u32[]{:S(2)}, u32[]{:S(2)}) collective-permute-start(bf16[34,2,64,128]{3,2,1,0:T(8,128)(2,1)} %collective-permute-done.refs_9_), channel_id=1, source_target_pairs={{0,1},{1,0},{2,3},{3,2},{4,5},{5,4},{6,7},{7,6}} | collective-permute-start | bytes 3342344 | tf_op jit(solution)/shard_map/cond/branch_0_fun/ppermute | solution.py:536
  43.5 116.6 %collective-permute-start.6 = (bf16[2,64,2048]{2,1,0:T(8,128)(2,1)}, bf16[2,64,2048]{2,1,0:T(8,128)(2,1)}, u32[]{:S(2)}, u32[]{:S(2)}) collective-permute-start(bf16[2,64,2048]{2,1,0:T(8,128)(2,1)} %get-tuple-element.116), channel_id=1, source_target_pairs={{0,2},{2,0},{1,3},{3,1},{4,6},{6,4},{5,7},{7,5}} | collective-permute-start | bytes 1572872 | tf_op jit(solution)/shard_map/cond/branch_0_fun/ppermute | solution.py:529
  47.9 112.2 %collective-permute-start.7 = (bf16[2,64,2048]{2,1,0:T(8,128)(2,1)}, bf16[2,64,2048]{2,1,0:T(8,128)(2,1)}, u32[]{:S(2)}, u32[]{:S(2)}) collective-permute-start(bf16[2,64,2048]{2,1,0:T(8,128)(2,1)} %get-tuple-element.117), channel_id=1, source_target_pairs={{0,2},{2,0},{1,3},{3,1},{4,6},{6,4},{5,7},{7,5}} | collective-permute-start | bytes 1572872 | tf_op jit(solution)/shard_map/cond/branch_0_fun/ppermute | solution.py:539
  67.3 48.6 %collective-permute-start.3 = (bf16[34,2,64,128]{3,2,1,0:T(8,128)(2,1)}, bf16[34,2,64,128]{3,2,1,0:T(8,128)(2,1)S(1)}, u32[]{:S(2)}, u32[]{:S(2)}) collective-permute-start(bf16[34,2,64,128]{3,2,1,0:T(8,128)(2,1)} %collective-permute-done.2.refs_9_), channel_id=1, source_target_pairs={{0,1},{1,0},{2,3},{3,2},{4,5},{5,4},{6,7},{7,6}} | collective-permute-start | bytes 3342344 | tf_op jit(solution)/shard_map/cond/branch_0_fun/ppermute | solution.py:536
  67.3 25.8 %copy-start.3 = (bf16[4,2048,128]{2,1,0:T(8,128)(2,1)S(1)}, bf16[4,2048,128]{2,1,0:T(8,128)(2,1)}, u32[]{:S(2)}) copy-start(bf16[4,2048,128]{2,1,0:T(8,128)(2,1)} %get-tuple-element.83.refs_5_.refs_17_) | copy-start | bytes 6291460 | tf_op jit(solution)/shard_map/cond
  91.1 69.0 %collective-permute-start.8 = (bf16[2,64,2048]{2,1,0:T(8,128)(2,1)}, bf16[2,64,2048]{2,1,0:T(8,128)(2,1)}, u32[]{:S(2)}, u32[]{:S(2)}) collective-permute-start(bf16[2,64,2048]{2,1,0:T(8,128)(2,1)} %get-tuple-element.118), channel_id=1, source_target_pairs={{0,3},{3,0},{1,2},{2,1},{4,7},{7,4},{5,6},{6,5}} | collective-permute-start | bytes 1572872 | tf_op jit(solution)/shard_map/cond/branch_0_fun/ppermute | solution.py:540
  91.1 47.6 %collective-permute-start.5 = (bf16[34,2,64,128]{3,2,1,0:T(8,128)(2,1)S(1)}, bf16[34,2,64,128]{3,2,1,0:T(8,128)(2,1)S(1)}, u32[]{:S(2)}, u32[]{:S(2)}) collective-permute-start(bf16[34,2,64,128]{3,2,1,0:T(8,128)(2,1)S(1)} %collective-permute-done.4.refs_9_), channel_id=1, source_target_pairs={{0,1},{1,0},{2,3},{3,2},{4,5},{5,4},{6,7},{7,6}} | collective-permute-start | bytes 3342344 | tf_op jit(solution)/shard_map/cond/branch_0_fun/ppermute | solution.py:536
  113.1 2.8 %copy-start.14 = (bf16[2,64,2048]{2,1,0:T(8,128)(2,1)S(1)}, bf16[2,64,2048]{2,1,0:T(8,128)(2,1)}, u32[]{:S(2)}) copy-start(bf16[2,64,2048]{2,1,0:T(8,128)(2,1)} %get-tuple-element.119) | copy-start | bytes 1572868 | tf_op jit(solution)/shard_map/cond
  115.9 1.0 copy-start.9
  115.9 44.1 %collective-permute-start.9 = (bf16[2,64,2048]{2,1,0:T(8,128)(2,1)S(1)}, bf16[2,64,2048]{2,1,0:T(8,128)(2,1)}, u32[]{:S(2)}, u32[]{:S(2)}) collective-permute-start(bf16[2,64,2048]{2,1,0:T(8,128)(2,1)S(1)} %copy-done.14), channel_id=1, source_target_pairs={{0,3},{3,0},{1,2},{2,1},{4,7},{7,4},{5,6},{6,5}} | collective-permute-start | bytes 1572872 | tf_op jit(solution)/shard_map/cond/branch_0_fun/ppermute | solution.py:541
  138.7 1.0 copy-start.8
  160.3 0.5 copy-start.13
  160.9 8.7 %copy-start.12 = (bf16[1,2048]{1,0:T(2,128)(2,1)S(1)}, bf16[1,2048]{1,0:T(2,128)(2,1)}, u32[]{:S(2)}) copy-start(bf16[1,2048]{1,0:T(2,128)(2,1)} %get-tuple-element.258.h_ref) | copy-start | bytes 12292

commit v2 on v1

--- a/solution.py
+++ b/solution.py
@@ -43,95 +43,87 @@
     return start, count
 
 
-def swap_kernel(layers, k_ref, v_ref, far_o, near_o, send_sem, recv_sem):
+def trade_kernel(layers, n_chunks, lengths, k_ref, v_ref, out_ref, near_o, both, own_sem, send_sem, recv_sem):
     sp, core, chip = place()
     peer = sp + 1 - 2 * core
+    layer = layers[0]
+    per_shard = SHARD // CHUNK
+    far_row = 2 * (1 - chip)
     barrier = pltpu.get_barrier_semaphore()
     pl.semaphore_signal(barrier, inc=1, device_id={"sp": peer}, device_id_type=pl.DeviceIdType.MESH)
-    pl.semaphore_wait(barrier, 1)
-    far_rows = pl.ds(2 * (1 - chip), 2)
 
     def send(src, dst, i):
         return pltpu.make_async_remote_copy(
             src_ref=src, dst_ref=dst, send_sem=send_sem.at[i], recv_sem=recv_sem.at[i],
             device_id={"sp": peer}, device_id_type=pl.DeviceIdType.MESH)
 
-    copies = []
-    for i, (layer, sliding) in enumerate(layers):
-        if sliding:
-            @pl.when(core == 0)
-            def _(layer=layer, i=i):
-                send(v_ref.at[layer, far_rows], far_o.at[i], 3 * i).start()
-
-            @pl.when(core == 1)
-            def _(layer=layer, i=i):
-                send(k_ref.at[layer, far_rows], far_o.at[i], 3 * i).start()
-
-            copies.append(send(k_ref.at[layer, far_rows], far_o.at[i], 3 * i))
-        pair = [send(k_ref.at[layer, peer], near_o.at[i, 0], 3 * i + 1),
-                send(v_ref.at[layer, peer], near_o.at[i, 1], 3 * i + 2)]
-        for copy in pair:
-            copy.start()
-        copies += pair
-    for copy in copies:
-        copy.wait()
-
-
-def swap(layers, k_t, v_t, collective_id):
-    n = len(layers)
-    block = jax.ShapeDtypeStruct((n, 2, 2, HEAD_DIM, SHARD), jnp.bfloat16)
-    return pl.pallas_call(
-        functools.partial(swap_kernel, layers),
-        out_shape=[block, block],
-        in_specs=[ANY, ANY], out_specs=[ANY, ANY],
-        scratch_shapes=[pltpu.SemaphoreType.DMA((3 * n,)), pltpu.SemaphoreType.DMA((3 * n,))],
-        compiler_params=params(60, collective_id=collective_id, has_side_effects=True),
-        cost_estimate=pl.CostEstimate(flops=10**9, bytes_accessed=4 * 2**20, transcendentals=0),
-        name="swap",
-    )(k_t, v_t)
-
-
-def pack_kernel(layer, n_chunks, lengths, k_ref, v_ref, recv_ref, out_ref, sem):
-    _, core, chip = place()
-    far_row = 2 * (1 - chip)
+    def chunk(ref, i):
+        return ref.at[layer, far_row + i // per_shard, :, :, pl.ds(pl.multiple_of(lax.rem(i, per_shard) * CHUNK, CHUNK), CHUNK)]
+
+    def spot(i):
+        return both.at[core * 2 * per_shard + i]
+
+    def load(i, carry):
+        @pl.when(core == 0)
+        def _():
+            pltpu.make_async_copy(chunk(k_ref, i), spot(i), own_sem).start()
+
+        @pl.when(core == 1)
+        def _():
+            pltpu.make_async_copy(chunk(v_ref, i), spot(i), own_sem).start()
+
+        return carry
+
+    def give(i, carry):
+        @pl.when(core == 0)
+        def _():
+            send(chunk(v_ref, i), spot(i), 0).start()
+
+        @pl.when(core == 1)
+        def _():
+            send(chunk(k_ref, i), spot(i), 0).start()
+
+        return carry
+
+    pl.semaphore_wait(barrier, 1)
+    lax.fori_loop(0, 2 * per_shard, give, 0)
+    lax.fori_loop(0, 2 * per_shard, load, 0)
+    nears = [send(ref.at[layers[i // 2], peer], near_o.at[i // 2, i % 2], 1 + i)
+             for i, ref in enumerate((k_ref, v_ref) * len(layers))]
+    for copy in nears:
+        copy.start()
     start0, count0 = far_chunks(lengths[far_row], chip == 1)
     start1, _ = far_chunks(lengths[far_row + 1], chip == 1)
-    per_shard = SHARD // CHUNK
+    half = pl.ds(core * 2 * per_shard, 2 * per_shard)
+    other = pl.ds((1 - core) * 2 * per_shard, 2 * per_shard)
+    pltpu.make_async_copy(both.at[half], both.at[half], own_sem).wait()
+    send(both.at[half], both.at[other], 0).wait_recv()
 
     def step(j, carry):
         second = j >= count0
-        row = jnp.where(second, 1, 0)
         piece = jnp.clip(jnp.where(second, start1 + j - count0, start0 + j), 0, 2 * per_shard - 1)
-        own = (piece // per_shard) == core
-        lanes = pl.ds(pl.multiple_of(lax.rem(piece, per_shard) * CHUNK, CHUNK), CHUNK)
-
-        @pl.when(own & (core == 0))
-        def _():
-            pltpu.make_async_copy(k_ref.at[layer, far_row + row, :, :, lanes], out_ref.at[j], sem).start()
-
-        @pl.when(own & (core == 1))
-        def _():
-            pltpu.make_async_copy(v_ref.at[layer, far_row + row, :, :, lanes], out_ref.at[j], sem).start()
-
-        @pl.when(jnp.logical_not(own))
-        def _():
-            pltpu.make_async_copy(recv_ref.at[0, row, :, :, lanes], out_ref.at[j], sem).start()
-
+        out_ref[j] = both[piece + jnp.where(piece >= per_shard, per_shard, 0) + jnp.where(second, per_shard, 0)]
         return carry
 
     lax.fori_loop(0, n_chunks, step, 0)
-    pltpu.make_async_copy(out_ref, out_ref, sem).wait()
-
-
-def pack(layer, n_chunks, lengths, k_t, v_t, recv):
+    send(both.at[half], both.at[other], 0).wait_send()
+    for copy in nears:
+        copy.wait()
+
+
+def trade(layers, n_chunks, lengths, k_t, v_t):
+    n = len(layers)
+    n_copies = 1 + 2 * n
     return pl.pallas_call(
-        functools.partial(pack_kernel, layer, n_chunks),
-        out_shape=jax.ShapeDtypeStruct((n_chunks, 2, HEAD_DIM, CHUNK), jnp.bfloat16),
-        in_specs=[SMEM, ANY, ANY, ANY], out_specs=VMEM,
-        scratch_shapes=[pltpu.SemaphoreType.DMA],
-        compiler_params=params(60),
-        cost_estimate=pl.CostEstimate(flops=10**9, bytes_accessed=4 * 2**20, transcendentals=0),
-    )(lengths, k_t, v_t, recv)
+        functools.partial(trade_kernel, layers, n_chunks),
+        out_shape=[jax.ShapeDtypeStruct((n_chunks, 2, HEAD_DIM, CHUNK), jnp.bfloat16),
+                   jax.ShapeDtypeStruct((n, 2, 2, HEAD_DIM, SHARD), jnp.bfloat16)],
+        in_specs=[SMEM, ANY, ANY], out_specs=[VMEM, ANY],
+        scratch_shapes=[pltpu.VMEM((4 * SHARD // CHUNK, 2, HEAD_DIM, CHUNK), jnp.bfloat16), pltpu.SemaphoreType.DMA,
+                        pltpu.SemaphoreType.DMA((n_copies,)), pltpu.SemaphoreType.DMA((n_copies,))],
+        compiler_params=params(60, collective_id=2 + 6 * SIZES.index(n_chunks) + layers[0], has_side_effects=True),
+        cost_estimate=pl.CostEstimate(flops=10**9, bytes_accessed=6 * 2**20, transcendentals=0),
+    )(lengths, k_t, v_t)
 
 
 def payload_kernel(layer, picks, k_ref, v_ref, *refs):
@@ -293,6 +285,28 @@
         compiler_params=params(4, collective_id=1, has_side_effects=True),
         name="final",
     )(h, part)
+
+
+def open_kernel(layer, lengths, k_ref, v_ref, same_o, choice_o, sem):
+    sp, _, chip = place()
+    copy = pltpu.make_async_copy(k_ref.at[layer, sp + 2 - 4 * chip], same_o, sem)
+    copy.start()
+    counts = [far_chunks(lengths[row], row < 2)[1] for row in range(4)]
+    needed = jnp.maximum(counts[0] + counts[1], counts[2] + counts[3])
+    choice_o[0] = sum(jnp.where(needed > size, 1, 0) for size in SIZES[:-1])
+    copy.wait()
+
+
+def open_step(layer, lengths, k_t, v_t):
+    return pl.pallas_call(
+        functools.partial(open_kernel, layer),
+        out_shape=[jax.ShapeDtypeStruct((2, HEAD_DIM, SHARD), jnp.bfloat16), jax.ShapeDtypeStruct((1,), jnp.int32)],
+        in_specs=[SMEM, ANY, ANY], out_specs=[VMEM, SMEM],
+        scratch_shapes=[pltpu.SemaphoreType.DMA],
+        compiler_params=params(60),
+        cost_estimate=pl.CostEstimate(flops=10**9, bytes_accessed=2**20, transcendentals=0),
+        name="open",
+    )(lengths, k_t, v_t)
 
 
 def as_column(row, base):
@@ -529,9 +543,7 @@
     same_k = lax.ppermute(same_k, "sp", CROSS)
     streams = []
     for layer in range(last):
-        traded = ((layer, True),) if layer < last - 1 else ((layer, True), (last, False))
-        far, near = swap(traded, k_t, v_t, 2 + layer)
-        packed = pack(layer, n_chunks, lengths, k_t, v_t, far)
+        packed, near = trade((layer,) if layer < last - 1 else (layer, last), n_chunks, lengths, k_t, v_t)
         mine = lax.ppermute(packed, "sp", CROSS)
         other = lax.ppermute(mine, "sp", PARTNER)
         streams.append((near, mine, other))
@@ -561,9 +573,7 @@
 def decode(k_t, v_t, lengths, hidden, ln_gain, w_query, w_key, w_value, w_out, w_gate, w_up, w_down):
     weights = (w_query, w_key, w_value, w_gate, w_up, w_down)
 
-    counts = far_chunks(lengths, jnp.arange(4) < 2)[1]
-    needed = jnp.maximum(counts[0] + counts[1], counts[2] + counts[3])
-    choice = sum((needed > size).astype(jnp.int32) for size in SIZES[:-1])
+    same_k, choice = open_step(w_out.shape[0] - 1, lengths, k_t, v_t)
 
     def branch(i):
         def run(args):
@@ -571,16 +581,15 @@
 
         return run
 
-    (same_k,) = payload(w_out.shape[0] - 1, (("same", 0),), k_t, v_t)
     args = (same_k, k_t, v_t, lengths, hidden, ln_gain, weights, w_out)
-    state, pieces, windows, outs = lax.switch(choice, [branch(i) for i in range(len(SIZES))], args)
+    state, pieces, windows, outs = lax.switch(choice[0], [branch(i) for i in range(len(SIZES))], args)
     *inputs, residual = state
     part, *caches = global_layer(w_out.shape[0] - 1, lengths, *inputs, k_t, v_t, pieces, w_out, windows, outs)
     global_k, global_v, window_k, window_v = caches
     return final(residual, part), window_k, window_v, global_k, global_v
 
 
-SIZES = (34, 50, 64)
+SIZES = (34, 45, 55, 64)
 
 
 def solution(mesh):

time: 175 us -> 172 us (0.983)
  Pallas kernels: 127 us -> 121 us
  waiting for transfers between devices: 31.2 us -> 34.9 us
  starting transfers between devices: 7.12 us -> 9.15 us
  between operations: 3.35 us -> 1.39 us
    pallas_call x6 -> x4, Pallas kernels: 28.4 us -> 23.1 us  [the longest x3 20.4 us: trade(): pl.pallas_call(functools.partial(trade_kernel, layers, n_chunks), out_sha...]
    ppermute x3, waiting for transfers between devices: 31.2 us -> 34.9 us  [run_layers(): mine = lax.ppermute(packed, 'sp', CROSS)]
    ppermute x3, starting transfers between devices: 2.32 us -> 4.93 us  [run_layers(): mine = lax.ppermute(packed, 'sp', CROSS)]
    pallas_call x2 -> x1, Pallas kernels: 4.53 us -> 2.55 us  [payload(): pl.pallas_call(functools.partial(payload_kernel, layer, picks), out_shape...]
  transfers between devices with their start and end apart: 10 -> 10, of which waited for: 3 -> 3; matrix products, arithmetic and copies ran while one was open for 1% -> 1% of each run, Pallas kernels for 59% -> 57%
where the time goes in v2:
time: 172 us
  Pallas kernels  121 us (70%)
  waiting for transfers between devices  34.9 us (20%)
  starting transfers between devices  9.15 us (5%)
  local copies, waits for them, and re-layouts  3.83 us (2%)
    pallas_call x3, Pallas kernels, sliding_layer(): pl.pallas_call(functools.partial(layer_kernel, layer, sliding_next), out_...  59.3 us
    ppermute x3, waiting for transfers between devices, run_layers(): mine = lax.ppermute(packed, 'sp', CROSS)  34.9 us
    pallas_call x3, Pallas kernels, trade(): pl.pallas_call(functools.partial(trade_kernel, layers, n_chunks), out_sha...  20.4 us
    pallas_call x1, Pallas kernels, front(): pl.pallas_call(front_kernel, out_shape=out, in_specs=[VMEM] * 4 + [ANY] *...  16.2 us
    pallas_call x1, Pallas kernels, global_layer(): pl.pallas_call(functools.partial(global_kernel, layer), out_shape=[jax.Sh...  10.4 us
    pallas_call x2, Pallas kernels, emit(): pl.pallas_call(functools.partial(emit_kernel, layer), out_shape=[out, out...  5.4 us
    ppermute x3, starting transfers between devices, run_layers(): mine = lax.ppermute(packed, 'sp', CROSS)  4.93 us
    pallas_call x1, Pallas kernels, final(): pl.pallas_call(final_kernel, out_shape=jax.ShapeDtypeStruct(h.shape, jnp....  3.7 us
  transfers between devices with their start and end apart: 10, of which 3 were waited for; matrix products, arithmetic and copies ran while one was open for 1% of the time, Pallas kernels for 57%

profile of v2, /device:TPU:0, one launch (start us, length us, event | category | flops | bytes accessed | tf_op | source)
XLA Modules:
  0.0 171.7 jit_solution(13358252537450651854)
XLA Ops:
  0.7 2.7 %open.1 = (bf16[2,64,2048]{2,1,0:T(8,128)(2,1)}, s32[1]{0:T(128)}) custom-call(s32[4]{0:T(128)} %lengths.3, bf16[4,4,2,64,2048]{4,3,2,1,0:T(8,128)(2,1)} %bitcast.23, bf16[4,4,2,64,2048]{4,3,2,1,0:T(8,128)(2,1)} %bitcast.29), custom_call_target="tpu_custom_call" | custom-call | flops 1000000000 | bytes 1048576 | tf_op jit(solution)/shard_map/open/pallas_call | solution.py:301
  4.0 152.4 %conditional.1 = (bf16[1,1024]{1,0:T(2,128)(2,1)S(1)}, bf16[1,128]{1,0:T(2,128)(2,1)S(1)}, bf16[1,128]{1,0:T(2,128)(2,1)}, f32[1,2048]{1,0:T(1,128)S(1)}, bf16[1...) conditional(s32[]{:T(128)} %bitcast.6, (s32[4]{0:T(128)S(1)}, ...), branch_computations={%region_0.0_spmd, %region_1.0_spmd, %region_2.0_spmd, %region_3.0_... | conditional | flops 36000002048 | bytes 316832704 | solution.py:585
  4.0 6.6 %branch_0_fun.8 = (bf16[34,2,64,128]{3,2,1,0:T(8,128)(2,1)}, bf16[1,2,2,64,2048]{4,3,2,1,0:T(8,128)(2,1)}) custom-call(s32[4]{0:T(128)S(1)} %get-tuple-element.104.lengths.refs_0_, bf16[4,4,2,64,2048]{4,3,2,1,0:T(8,128)(2,1)} %get-tuple-element.118.k_ref.refs_6_, bf16[4,4,2,64,2048]{4,3,2,1,0:T(8,128)(2,1)} %get-tuple-element.119.v_ref.refs_7_), custom_call_target="tpu_custom_call" | custom-call | flops 1000000000 | bytes 6291456 | tf_op jit(solution)/shard_map/cond/branch_0_fun/pallas_call | solution.py:117
  10.6 2.9 %collective-permute-start = (bf16[34,2,64,128]{3,2,1,0:T(8,128)(2,1)}, bf16[34,2,64,128]{3,2,1,0:T(8,128)(2,1)}, u32[]{:S(2)}, u32[]{:S(2)}) collective-permute-start(bf16[34,2,64,128]{3,2,1,0:T(8,128)(2,1)} %get-tuple-element.121), channel_id=1, source_target_pairs={{0,2},{2,0},{1,3},{3,1},{4,6},{6,4},{5,7},{7,5}} | collective-permute-start | bytes 3342344 | tf_op jit(solution)/shard_map/cond/branch_0_fun/ppermute | solution.py:547
  13.5 6.2 %branch_0_fun.10 = (bf16[34,2,64,128]{3,2,1,0:T(8,128)(2,1)}, bf16[1,2,2,64,2048]{4,3,2,1,0:T(8,128)(2,1)}) custom-call(s32[4]{0:T(128)S(1)} %get-tuple-element.104.lengths.refs_0_, bf16[4,4,2,64,2048]{4,3,2,1,0:T(8,128)(2,1)} %get-tuple-element.118.k_ref.refs_6_, bf16[4,4,2,64,2048]{4,3,2,1,0:T(8,128)(2,1)} %get-tuple-element.119.v_ref.refs_7_), custom_call_target="tpu_custom_call" | custom-call | flops 1000000000 | bytes 6291456 | tf_op jit(solution)/shard_map/cond/branch_0_fun/pallas_call | solution.py:117
  19.7 7.7 %branch_0_fun.12 = (bf16[34,2,64,128]{3,2,1,0:T(8,128)(2,1)}, bf16[2,2,2,64,2048]{4,3,2,1,0:T(8,128)(2,1)}) custom-call(s32[4]{0:T(128)S(1)} %get-tuple-element.104.lengths.refs_0_, bf16[4,4,2,64,2048]{4,3,2,1,0:T(8,128)(2,1)} %get-tuple-element.118.k_ref.refs_6_, bf16[4,4,2,64,2048]{4,3,2,1,0:T(8,128)(2,1)} %get-tuple-element.119.v_ref.refs_7_), custom_call_target="tpu_custom_call" | custom-call | flops 1000000000 | bytes 6291456 | tf_op jit(solution)/shard_map/cond/branch_0_fun/pallas_call | solution.py:117
  27.4 2.0 %collective-permute-start.4 = (bf16[34,2,64,128]{3,2,1,0:T(8,128)(2,1)}, bf16[34,2,64,128]{3,2,1,0:T(8,128)(2,1)S(1)}, u32[]{:S(2)}, u32[]{:S(2)}) collective-permute-start(bf16[34,2,64,128]{3,2,1,0:T(8,128)(2,1)} %get-tuple-element.136), channel_id=1, source_target_pairs={{0,2},{2,0},{1,3},{3,1},{4,6},{6,4},{5,7},{7,5}} | collective-permute-start | bytes 3342344 | tf_op jit(solution)/shard_map/cond/branch_0_fun/ppermute | solution.py:547
  29.4 9.8 %collective-permute-done.refs_9_ = bf16[34,2,64,128]{3,2,1,0:T(8,128)(2,1)} collective-permute-done((bf16[34,2,64,128]{3,2,1,0:T(8,128)(2,1)}, bf16[34,2,64,128]{3,2,1,0:T(8,128)(2,1)}, u32[]{:S(2)}, u32[]{:S(2)}) %collective-permute-start) | collective-permute-done | bytes 1114144 | tf_op jit(solution)/shard_map/cond/branch_0_fun/ppermute | solution.py:547
  39.2 2.0 %collective-permute-start.6 = (bf16[2,64,2048]{2,1,0:T(8,128)(2,1)}, bf16[2,64,2048]{2,1,0:T(8,128)(2,1)}, u32[]{:S(2)}, u32[]{:S(2)}) collective-permute-start(bf16[2,64,2048]{2,1,0:T(8,128)(2,1)} %get-tuple-element.142), channel_id=1, source_target_pairs={{0,2},{2,0},{1,3},{3,1},{4,6},{6,4},{5,7},{7,5}} | collective-permute-start | bytes 1572872 | tf_op jit(solution)/shard_map/cond/branch_0_fun/ppermute | solution.py:543
  41.2 2.6 %payload.4 = (bf16[2,64,2048]{2,1,0:T(8,128)(2,1)}, bf16[2,64,2048]{2,1,0:T(8,128)(2,1)}, bf16[2,64,2048]{2,1,0:T(8,128)(2,1)}) custom-call(bf16[4,4,2,64,2048]{4,3,2,1,0:T(8,128)(2,1)} %get-tuple-element.118.k_ref.refs_6_, bf16[4,4,2,64,2048]{4,3,2,1,0:T(8,128)(2,1)} %get-tuple-element.119.v_ref.refs_7_), custom_call_target="tpu_custom_call" | custom-call | flops 1000000000 | bytes 3145728 | tf_op jit(solution)/shard_map/cond/branch_0_fun/payload/pallas_call | solution.py:143
  43.9 0.6 dynamic_slice.8
  45.1 0.1 pad_maximum_fusion
  45.2 0.1 tile.25.refs_1_.refs_13_
  45.3 0.1 fusion.2
  45.4 0.1 pad_maximum_fusion.1
  45.5 0.1 tile.27.refs_2_.refs_14_
  45.5 17.6 %collective-permute-done.2.refs_9_ = bf16[34,2,64,128]{3,2,1,0:T(8,128)(2,1)} collective-permute-done((bf16[34,2,64,128]{3,2,1,0:T(8,128)(2,1)}, bf16[34,2,64,128]{3,2,1,0:T(8,128)(2,1)}, u32[]{:S(2)}, u32[]{:S(2)}) %collective-permute-start.2) | collective-permute-done | bytes 1114144 | tf_op jit(solution)/shard_map/cond/branch_0_fun/ppermute | solution.py:547
  63.1 16.2 %front.4 = (bf16[1,1024]{1,0:T(2,128)(2,1)S(1)}, bf16[1,128]{1,0:T(2,128)(2,1)S(1)}, bf16[1,128]{1,0:T(2,128)(2,1)S(1)}, f32[1,2048]{1,0:T(1,128)S(1)}, bf16[1,2048]{1,0:T(2,128)(2,1)S(1)}) custom-call(bf16[1,2048]{1,0:T(2,128)(2,1)S(1)} %get-tuple-element.105.h_ref, bf16[4,2048]{1,0:T(4,128)(2,1)S(1)} %get-tuple-element.106.refs_0_.refs_12_, ...), custom_call_target="tpu_custom_call" | custom-call | flops 6000000000 | bytes 40000000 | tf_op jit(solution)/shard_map/cond/branch_0_fun/front/pallas_call | solution.py:261
  79.3 7.5 %collective-permute-done.4.refs_9_ = bf16[34,2,64,128]{3,2,1,0:T(8,128)(2,1)S(1)} collective-permute-done((bf16[34,2,64,128]{3,2,1,0:T(8,128)(2,1)}, bf16[34,2,64,128]{3,2,1,0:T(8,128)(2,1)S(1)}, u32[]{:S(2)}, u32[]{:S(2)}) %collective-permute-start.4) | collective-permute-done | bytes 1114144 | tf_op jit(solution)/shard_map/cond/branch_0_fun/ppermute | solution.py:547
  86.9 0.1 collective-permute-start.8
  87.0 2.1 %collective-permute-start.5 = (bf16[34,2,64,128]{3,2,1,0:T(8,128)(2,1)S(1)}, bf16[34,2,64,128]{3,2,1,0:T(8,128)(2,1)S(1)}, u32[]{:S(2)}, u32[]{:S(2)}) collective-permute-start(bf16[34,2,64,128]{3,2,1,0:T(8,128)(2,1)S(1)} %collective-permute-done.4.refs_9_), channel_id=1, source_target_pairs={{0,1},{1,0},{2,3},{3,2},{4,5},{5,4},{6,7},{7,6}} | collective-permute-start | bytes 3342344 | tf_op jit(solution)/shard_map/cond/branch_0_fun/ppermute | solution.py:548
  89.0 20.1 %branch_0_fun.9 = (bf16[1,1024]{1,0:T(2,128)(2,1)S(1)}, bf16[1,128]{1,0:T(2,128)(2,1)S(1)}, bf16[1,128]{1,0:T(2,128)(2,1)S(1)}, f32[1,2048]{1,0:T(1,128)S(1)}, b...) custom-call(s32[4]{0:T(128)S(1)} %get-tuple-element.104.lengths.refs_0_, ...), custom_call_target="tpu_custom_call" | custom-call | flops 8000000000 | bytes 54525952 | tf_op jit(solution)/shard_map/cond/branch_0_fun/pallas_call | solution.py:434
  109.1 2.7 %branch_0_fun.14 = (bf16[3,2,64,4096]{3,2,1,0:T(8,128)(2,1)}, bf16[3,2,64,4096]{3,2,1,0:T(8,128)(2,1)}) custom-call(bf16[2,64,4096]{2,1,0:T(8,128)(2,1)S(1)} %get-tuple-element.150.wk_ref, bf16[2,64,4096]{2,1,0:T(8,128)(2,1)} %get-tuple-element.151.wv_ref), custom_call_target="tpu_custom_call" | custom-call | flops 1000000000 | bytes 4194304 | tf_op jit(solution)/shard_map/cond/branch_0_fun/pallas_call | solution.py:464
  111.9 0.9 copy-done.11
  112.8 19.1 %branch_0_fun.11 = (bf16[1,1024]{1,0:T(2,128)(2,1)S(1)}, bf16[1,128]{1,0:T(2,128)(2,1)S(1)}, bf16[1,128]{1,0:T(2,128)(2,1)S(1)}, f32[1,2048]{1,0:T(1,128)S(1)}, ...) custom-call(s32[4]{0:T(128)S(1)} %get-tuple-element.104.lengths.refs_0_, ...), custom_call_target="tpu_custom_call" | custom-call | flops 8000000000 | bytes 54525952 | tf_op jit(solution)/shard_map/cond/branch_0_fun/pallas_call | solution.py:434
  131.9 2.7 %branch_0_fun.15 = (bf16[3,2,64,4096]{3,2,1,0:T(8,128)(2,1)}, bf16[3,2,64,4096]{3,2,1,0:T(8,128)(2,1)}) custom-call(bf16[2,64,4096]{2,1,0:T(8,128)(2,1)S(1)} %get-tuple-element.148.wk_ref, bf16[2,64,4096]{2,1,0:T(8,128)(2,1)} %get-tuple-element.149.wv_ref, ...), custom_call_target="tpu_custom_call", output_to_operand_aliasing={{0}: (2, {}), {1}: (3, {})} | custom-call | flops 1000000000 | bytes 4194304 | tf_op jit(solution)/shard_map/cond/branch_0_fun/pallas_call | solution.py:464
  134.7 1.0 copy-done.10
  135.6 20.2 %branch_0_fun.13 = (bf16[1,1024]{1,0:T(2,128)(2,1)S(1)}, bf16[1,128]{1,0:T(2,128)(2,1)S(1)}, bf16[1,128]{1,0:T(2,128)(2,1)}, f32[1,2048]{1,0:T(1,128)S(1)}, bf16...) custom-call(s32[4]{0:T(128)S(1)} %get-tuple-element.104.lengths.refs_0_, ...), custom_call_target="tpu_custom_call" | custom-call | flops 8000000000 | bytes 54525952 | tf_op jit(solution)/shard_map/cond/branch_0_fun/pallas_call | solution.py:434
  156.4 0.5 copy-done.15
  156.9 10.4 %global.1 = (f32[1,2048]{1,0:T(1,128)S(1)}, bf16[2,64,8192]{2,1,0:T(8,128)(2,1)}, bf16[2,64,8192]{2,1,0:T(8,128)(2,1)}, bf16[3,2,64,4096]{3,2,1,0:T(8,128)(2,1)}, bf16[3,2,64,4096]{3,2,1,0:T(8,128)(2,1)}) custom-call(s32[4]{0:T(128)S(1)} %copy-done.12, bf16[1,1024]{1,0:T(2,128)(2,1)S(1)} %get-tuple-element.341.q_ref, ...), custom_call_target="tpu_custom_call", output_to_operand_aliasing={{3}: (15, {}), {4}: (16, {})} | custom-call | flops 3000000000 | bytes 27262976 | tf_op jit(solution)/shard_map/global/pallas_call | solution.py:527
  167.4 3.7 %final.1 = bf16[1,2048]{1,0:T(2,128)(2,1)S(1)} custom-call(bf16[1,2048]{1,0:T(2,128)(2,1)S(1)} %copy-done.14, f32[1,2048]{1,0:T(1,128)S(1)} %get-tuple-element.354.part_ref), custom_call_target="tpu_custom_call" | custom-call | tf_op jit(solution)/shard_map/final/pallas_call | solution.py:280
  171.1 0.6 copy.96
  (32 shorter events, 0.2 us)
Async XLA Ops:
  0.6 3.4 %copy-start = (bf16[4,2048,128]{2,1,0:T(8,128)(2,1)S(1)}, bf16[4,2048,128]{2,1,0:T(8,128)(2,1)}, u32[]{:S(2)}) copy-start(bf16[4,2048,128]{2,1,0:T(8,128)(2,1)} %param.22) | copy-start | bytes 6291460
  0.6 3.4 %copy-start.7 = (bf16[4,2048]{1,0:T(4,128)(2,1)S(1)}, bf16[4,2048]{1,0:T(4,128)(2,1)}, u32[]{:S(2)}) copy-start(bf16[4,2048]{1,0:T(4,128)(2,1)} %param.20) | copy-start | bytes 49156
  0.7 3.4 %copy-start.12 = (s32[4]{0:T(128)S(1)}, s32[4]{0:T(128)}, u32[]{:S(2)}) copy-start(s32[4]{0:T(128)} %lengths.3) | copy-start | bytes 52
  0.7 3.4 %copy-start.13 = (bf16[1,2048]{1,0:T(2,128)(2,1)S(1)}, bf16[1,2048]{1,0:T(2,128)(2,1)}, u32[]{:S(2)}) copy-start(bf16[1,2048]{1,0:T(2,128)(2,1)} %param.19) | copy-start | bytes 12292
  10.6 28.6 %collective-permute-start = (bf16[34,2,64,128]{3,2,1,0:T(8,128)(2,1)}, bf16[34,2,64,128]{3,2,1,0:T(8,128)(2,1)}, u32[]{:S(2)}, u32[]{:S(2)}) collective-permute-start(bf16[34,2,64,128]{3,2,1,0:T(8,128)(2,1)} %get-tuple-element.121), channel_id=1, source_target_pairs={{0,2},{2,0},{1,3},{3,1},{4,6},{6,4},{5,7},{7,5}} | collective-permute-start | bytes 3342344 | tf_op jit(solution)/shard_map/cond/branch_0_fun/ppermute | solution.py:547
  19.7 43.4 %collective-permute-start.2 = (bf16[34,2,64,128]{3,2,1,0:T(8,128)(2,1)}, bf16[34,2,64,128]{3,2,1,0:T(8,128)(2,1)}, u32[]{:S(2)}, u32[]{:S(2)}) collective-permute-start(bf16[34,2,64,128]{3,2,1,0:T(8,128)(2,1)} %get-tuple-element.129), channel_id=1, source_target_pairs={{0,2},{2,0},{1,3},{3,1},{4,6},{6,4},{5,7},{7,5}} | collective-permute-start | bytes 3342344 | tf_op jit(solution)/shard_map/cond/branch_0_fun/ppermute | solution.py:547
  27.4 59.5 %collective-permute-start.4 = (bf16[34,2,64,128]{3,2,1,0:T(8,128)(2,1)}, bf16[34,2,64,128]{3,2,1,0:T(8,128)(2,1)S(1)}, u32[]{:S(2)}, u32[]{:S(2)}) collective-permute-start(bf16[34,2,64,128]{3,2,1,0:T(8,128)(2,1)} %get-tuple-element.136), channel_id=1, source_target_pairs={{0,2},{2,0},{1,3},{3,1},{4,6},{6,4},{5,7},{7,5}} | collective-permute-start | bytes 3342344 | tf_op jit(solution)/shard_map/cond/branch_0_fun/ppermute | solution.py:547
  39.2 47.7 %collective-permute-start.1 = (bf16[34,2,64,128]{3,2,1,0:T(8,128)(2,1)}, bf16[34,2,64,128]{3,2,1,0:T(8,128)(2,1)}, u32[]{:S(2)}, u32[]{:S(2)}) collective-permute-start(bf16[34,2,64,128]{3,2,1,0:T(8,128)(2,1)} %collective-permute-done.refs_9_), channel_id=1, source_target_pairs={{0,1},{1,0},{2,3},{3,2},{4,5},{5,4},{6,7},{7,6}} | collective-permute-start | bytes 3342344 | tf_op jit(solution)/shard_map/cond/branch_0_fun/ppermute | solution.py:548
  39.2 116.6 %collective-permute-start.6 = (bf16[2,64,2048]{2,1,0:T(8,128)(2,1)}, bf16[2,64,2048]{2,1,0:T(8,128)(2,1)}, u32[]{:S(2)}, u32[]{:S(2)}) collective-permute-start(bf16[2,64,2048]{2,1,0:T(8,128)(2,1)} %get-tuple-element.142), channel_id=1, source_target_pairs={{0,2},{2,0},{1,3},{3,1},{4,6},{6,4},{5,7},{7,5}} | collective-permute-start | bytes 1572872 | tf_op jit(solution)/shard_map/cond/branch_0_fun/ppermute | solution.py:543
  43.8 112.0 %collective-permute-start.7 = (bf16[2,64,2048]{2,1,0:T(8,128)(2,1)}, bf16[2,64,2048]{2,1,0:T(8,128)(2,1)}, u32[]{:S(2)}, u32[]{:S(2)}) collective-permute-start(bf16[2,64,2048]{2,1,0:T(8,128)(2,1)} %get-tuple-element.143), channel_id=1, source_target_pairs={{0,2},{2,0},{1,3},{3,1},{4,6},{6,4},{5,7},{7,5}} | collective-permute-start | bytes 1572872 | tf_op jit(solution)/shard_map/cond/branch_0_fun/ppermute | solution.py:551
  63.1 48.7 %collective-permute-start.3 = (bf16[34,2,64,128]{3,2,1,0:T(8,128)(2,1)}, bf16[34,2,64,128]{3,2,1,0:T(8,128)(2,1)S(1)}, u32[]{:S(2)}, u32[]{:S(2)}) collective-permute-start(bf16[34,2,64,128]{3,2,1,0:T(8,128)(2,1)} %collective-permute-done.2.refs_9_), channel_id=1, source_target_pairs={{0,1},{1,0},{2,3},{3,2},{4,5},{5,4},{6,7},{7,6}} | collective-permute-start | bytes 3342344 | tf_op jit(solution)/shard_map/cond/branch_0_fun/ppermute | solution.py:548
  63.1 25.9 %copy-start.3 = (bf16[4,2048,128]{2,1,0:T(8,128)(2,1)S(1)}, bf16[4,2048,128]{2,1,0:T(8,128)(2,1)}, u32[]{:S(2)}) copy-start(bf16[4,2048,128]{2,1,0:T(8,128)(2,1)} %get-tuple-element.109.refs_5_.refs_17_) | copy-start | bytes 6291460 | tf_op jit(solution)/shard_map/cond
  86.9 69.0 %collective-permute-start.8 = (bf16[2,64,2048]{2,1,0:T(8,128)(2,1)}, bf16[2,64,2048]{2,1,0:T(8,128)(2,1)}, u32[]{:S(2)}, u32[]{:S(2)}) collective-permute-start(bf16[2,64,2048]{2,1,0:T(8,128)(2,1)} %get-tuple-element.144), channel_id=1, source_target_pairs={{0,3},{3,0},{1,2},{2,1},{4,7},{7,4},{5,6},{6,5}} | collective-permute-start | bytes 1572872 | tf_op jit(solution)/shard_map/cond/branch_0_fun/ppermute | solution.py:552
  87.0 47.7 %collective-permute-start.5 = (bf16[34,2,64,128]{3,2,1,0:T(8,128)(2,1)S(1)}, bf16[34,2,64,128]{3,2,1,0:T(8,128)(2,1)S(1)}, u32[]{:S(2)}, u32[]{:S(2)}) collective-permute-start(bf16[34,2,64,128]{3,2,1,0:T(8,128)(2,1)S(1)} %collective-permute-done.4.refs_9_), channel_id=1, source_target_pairs={{0,1},{1,0},{2,3},{3,2},{4,5},{5,4},{6,7},{7,6}} | collective-permute-start | bytes 3342344 | tf_op jit(solution)/shard_map/cond/branch_0_fun/ppermute | solution.py:548
  109.1 2.8 %copy-start.16 = (bf16[2,64,2048]{2,1,0:T(8,128)(2,1)S(1)}, bf16[2,64,2048]{2,1,0:T(8,128)(2,1)}, u32[]{:S(2)}) copy-start(bf16[2,64,2048]{2,1,0:T(8,128)(2,1)} %get-tuple-element.145) | copy-start | bytes 1572868 | tf_op jit(solution)/shard_map/cond
  111.8 1.0 copy-start.11
  111.8 44.0 %collective-permute-start.9 = (bf16[2,64,2048]{2,1,0:T(8,128)(2,1)S(1)}, bf16[2,64,2048]{2,1,0:T(8,128)(2,1)}, u32[]{:S(2)}, u32[]{:S(2)}) collective-permute-start(bf16[2,64,2048]{2,1,0:T(8,128)(2,1)S(1)} %copy-done.16), channel_id=1, source_target_pairs={{0,3},{3,0},{1,2},{2,1},{4,7},{7,4},{5,6},{6,5}} | collective-permute-start | bytes 1572872 | tf_op jit(solution)/shard_map/cond/branch_0_fun/ppermute | solution.py:553
  134.6 1.0 copy-start.10
  156.4 0.5 copy-start.15
  156.9 10.4 %copy-start.14 = (bf16[1,2048]{1,0:T(2,128)(2,1)S(1)}, bf16[1,2048]{1,0:T(2,128)(2,1)}, u32[]{:S(2)}) copy-start(bf16[1,2048]{1,0:T(2,128)(2,1)} %get-tuple-element.340.h_ref) | copy-start | bytes 12292

commit v3 on v2

--- a/solution.py
+++ b/solution.py
@@ -43,7 +43,7 @@
     return start, count
 
 
-def trade_kernel(layers, n_chunks, lengths, k_ref, v_ref, out_ref, near_o, both, own_sem, send_sem, recv_sem):
+def trade_kernel(layers, n_chunks, lengths, k_ref, v_ref, out_ref, near_o, both, packed, own_sem, out_sem, send_sem, recv_sem):
     sp, core, chip = place()
     peer = sp + 1 - 2 * core
     layer = layers[0]
@@ -102,13 +102,16 @@
     def step(j, carry):
         second = j >= count0
         piece = jnp.clip(jnp.where(second, start1 + j - count0, start0 + j), 0, 2 * per_shard - 1)
-        out_ref[j] = both[piece + jnp.where(piece >= per_shard, per_shard, 0) + jnp.where(second, per_shard, 0)]
+        packed[j] = both[piece + jnp.where(piece >= per_shard, per_shard, 0) + jnp.where(second, per_shard, 0)]
         return carry
 
     lax.fori_loop(0, n_chunks, step, 0)
+    out = pltpu.make_async_copy(packed, out_ref, out_sem)
+    out.start()
     send(both.at[half], both.at[other], 0).wait_send()
     for copy in nears:
         copy.wait()
+    out.wait()
 
 
 def trade(layers, n_chunks, lengths, k_t, v_t):
@@ -118,8 +121,10 @@
         functools.partial(trade_kernel, layers, n_chunks),
         out_shape=[jax.ShapeDtypeStruct((n_chunks, 2, HEAD_DIM, CHUNK), jnp.bfloat16),
                    jax.ShapeDtypeStruct((n, 2, 2, HEAD_DIM, SHARD), jnp.bfloat16)],
-        in_specs=[SMEM, ANY, ANY], out_specs=[VMEM, ANY],
-        scratch_shapes=[pltpu.VMEM((4 * SHARD // CHUNK, 2, HEAD_DIM, CHUNK), jnp.bfloat16), pltpu.SemaphoreType.DMA,
+        in_specs=[SMEM, ANY, ANY], out_specs=[ANY, ANY],
+        scratch_shapes=[pltpu.VMEM((4 * SHARD // CHUNK, 2, HEAD_DIM, CHUNK), jnp.bfloat16),
+                        pltpu.VMEM((n_chunks, 2, HEAD_DIM, CHUNK), jnp.bfloat16),
+                        pltpu.SemaphoreType.DMA, pltpu.SemaphoreType.DMA,
                         pltpu.SemaphoreType.DMA((n_copies,)), pltpu.SemaphoreType.DMA((n_copies,))],
         compiler_params=params(60, collective_id=2 + 6 * SIZES.index(n_chunks) + layers[0], has_side_effects=True),
         cost_estimate=pl.CostEstimate(flops=10**9, bytes_accessed=6 * 2**20, transcendentals=0),
@@ -474,11 +479,7 @@
 
 
 def global_kernel(layer, lengths, q_ref, knew_ref, vnew_ref, mlp_ref, k_ref, v_ref, near_ref, *refs):
-    pieces = refs[:4]
-    (wo, wk_ref, wv_ref, _, _, part_o, gk_o, gv_o, wk_o, wv_o, k_buf, v_buf, wo_b, w_buf, load_sem, wo_sem, out_sem,
-     pass_in, pass_out) = refs[4:]
-    arrivals = [pltpu.make_async_copy(ref, w_buf.at[i], pass_in.at[i]) for i, ref in enumerate((wk_ref, wv_ref))]
-    departures = [pltpu.make_async_copy(w_buf.at[i], ref.at[layer - 1], pass_out.at[i]) for i, ref in enumerate((wk_o, wv_o))]
+    pieces, (wo, part_o, gk_o, gv_o, k_buf, v_buf, wo_b, load_sem, wo_sem, out_sem) = refs[:4], refs[4:]
     row, core, chip = place()
     last = lengths[row]
     across = row + 2 - 4 * chip
@@ -491,8 +492,6 @@
         copy.start()
     wo_copy = pltpu.make_async_copy(wo.at[layer], wo_b, wo_sem)
     wo_copy.start()
-    for copy in arrivals:
-        copy.start()
     k_new = [as_column(knew_ref[...], head * HEAD_DIM) for head in range(2)]
     v_new = [as_column(vnew_ref[...], head * HEAD_DIM) for head in range(2)]
     for copy in loads:
@@ -512,30 +511,24 @@
     stores = [pltpu.make_async_copy(k_buf, gk_o, out_sem.at[0]), pltpu.make_async_copy(v_buf, gv_o, out_sem.at[1])]
     for copy in stores:
         copy.start()
-    for arrival, departure in zip(arrivals, departures):
-        arrival.wait()
-        departure.start()
     attend(q_ref, k_buf, v_buf, last, wo_b, wo_copy, mlp_ref, part_o)
-    for copy in stores + departures:
+    for copy in stores:
         copy.wait()
 
 
-def global_layer(layer, lengths, q, k_new, v_new, mlp, k_t, v_t, pieces, wo, windows, outs):
+def global_layer(layer, lengths, q, k_new, v_new, mlp, k_t, v_t, pieces, wo):
     buf = pltpu.VMEM((2, HEAD_DIM, 4 * SHARD), jnp.bfloat16)
     out = jax.ShapeDtypeStruct((2, HEAD_DIM, 4 * SHARD), jnp.bfloat16)
-    window = jax.ShapeDtypeStruct(outs[0].shape, jnp.bfloat16)
     return pl.pallas_call(
         functools.partial(global_kernel, layer),
-        out_shape=[jax.ShapeDtypeStruct(mlp.shape, jnp.float32), out, out, window, window],
-        in_specs=[SMEM] + [VMEM] * 4 + [ANY] * 12, out_specs=[VMEM] + [ANY] * 4,
-        scratch_shapes=[buf, buf, pltpu.VMEM(wo.shape[1:], jnp.bfloat16), pltpu.VMEM((2,) + windows[0].shape, jnp.bfloat16),
-                        pltpu.SemaphoreType.DMA((8,)), pltpu.SemaphoreType.DMA, pltpu.SemaphoreType.DMA((2,)),
-                        pltpu.SemaphoreType.DMA((2,)), pltpu.SemaphoreType.DMA((2,))],
-        input_output_aliases={15: 3, 16: 4},
+        out_shape=[jax.ShapeDtypeStruct(mlp.shape, jnp.float32), out, out],
+        in_specs=[SMEM] + [VMEM] * 4 + [ANY] * 8, out_specs=[VMEM, ANY, ANY],
+        scratch_shapes=[buf, buf, pltpu.VMEM(wo.shape[1:], jnp.bfloat16), pltpu.SemaphoreType.DMA((8,)),
+                        pltpu.SemaphoreType.DMA, pltpu.SemaphoreType.DMA((2,))],
         compiler_params=params(),
-        cost_estimate=pl.CostEstimate(flops=3 * 10**9, bytes_accessed=26 * 2**20, transcendentals=0),
+        cost_estimate=pl.CostEstimate(flops=3 * 10**9, bytes_accessed=14 * 2**20, transcendentals=0),
         name="global",
-    )(lengths, q, k_new, v_new, mlp, k_t, v_t, *pieces, wo, *windows, *outs)
+    )(lengths, q, k_new, v_new, mlp, k_t, v_t, *pieces, wo)
 
 
 def run_layers(n_chunks, same_k, k_t, v_t, lengths, residual, ln_gain, weights, w_out):
@@ -565,9 +558,8 @@
     for layer in range(last):
         state, windows = sliding_layer(layer, layer + 1 < last, lengths, state, k_t, v_t, *streams[layer], w_out,
                                        ln_gain, cos, sin, weights)
-        if layer + 1 < last:
-            outs = emit(layer, windows, outs)
-    return state, (near, same_k, same_v, cross_k, cross_v), windows, outs
+        outs = emit(layer, windows, outs)
+    return state, (near, same_k, same_v, cross_k, cross_v), outs
 
 
 def decode(k_t, v_t, lengths, hidden, ln_gain, w_query, w_key, w_value, w_out, w_gate, w_up, w_down):
@@ -582,11 +574,10 @@
         return run
 
     args = (same_k, k_t, v_t, lengths, hidden, ln_gain, weights, w_out)
-    state, pieces, windows, outs = lax.switch(choice[0], [branch(i) for i in range(len(SIZES))], args)
+    state, pieces, outs = lax.switch(choice[0], [branch(i) for i in range(len(SIZES))], args)
     *inputs, residual = state
-    part, *caches = global_layer(w_out.shape[0] - 1, lengths, *inputs, k_t, v_t, pieces, w_out, windows, outs)
-    global_k, global_v, window_k, window_v = caches
-    return final(residual, part), window_k, window_v, global_k, global_v
+    part, global_k, global_v = global_layer(w_out.shape[0] - 1, lengths, *inputs, k_t, v_t, pieces, w_out)
+    return final(residual, part), outs[0], outs[1], global_k, global_v
 
 
 SIZES = (34, 45, 55, 64)

time: 172 us -> 171 us (level)
  Pallas kernels: 121 us -> 118 us
  waiting for transfers between devices: 34.9 us -> 37 us
    pallas_call x3, Pallas kernels: 20.4 us -> 17.4 us  [trade(): pl.pallas_call(functools.partial(trade_kernel, layers, n_chunks), out_sha...]
    pallas_call x2 -> x3, Pallas kernels: 5.4 us -> 8.14 us  [emit(): pl.pallas_call(functools.partial(emit_kernel, layer), out_shape=[out, out...]
    pallas_call x1, Pallas kernels: 10.4 us -> 7.71 us  [global_layer(): pl.pallas_call(functools.partial(global_kernel, layer), out_shape=[jax.Sh...]
    ppermute x3, waiting for transfers between devices: 34.9 us -> 36.9 us  [run_layers(): mine = lax.ppermute(packed, 'sp', CROSS)]
where the time goes in v3:
time: 171 us
  Pallas kernels  118 us (69%)
  waiting for transfers between devices  37 us (22%)
  starting transfers between devices  9.15 us (5%)
  local copies, waits for them, and re-layouts  3.83 us (2%)
    pallas_call x3, Pallas kernels, sliding_layer(): pl.pallas_call(functools.partial(layer_kernel, layer, sliding_next), out_...  59.2 us
    ppermute x3, waiting for transfers between devices, run_layers(): mine = lax.ppermute(packed, 'sp', CROSS)  36.9 us
    pallas_call x3, Pallas kernels, trade(): pl.pallas_call(functools.partial(trade_kernel, layers, n_chunks), out_sha...  17.4 us
    pallas_call x1, Pallas kernels, front(): pl.pallas_call(front_kernel, out_shape=out, in_specs=[VMEM] * 4 + [ANY] *...  16.2 us
    pallas_call x3, Pallas kernels, emit(): pl.pallas_call(functools.partial(emit_kernel, layer), out_shape=[out, out...  8.14 us
    pallas_call x1, Pallas kernels, global_layer(): pl.pallas_call(functools.partial(global_kernel, layer), out_shape=[jax.Sh...  7.71 us
    ppermute x3, starting transfers between devices, run_layers(): mine = lax.ppermute(packed, 'sp', CROSS)  4.93 us
    pallas_call x1, Pallas kernels, final(): pl.pallas_call(final_kernel, out_shape=jax.ShapeDtypeStruct(h.shape, jnp....  3.7 us
  transfers between devices with their start and end apart: 10, of which 3 were waited for; matrix products, arithmetic and copies ran while one was open for 1% of the time, Pallas kernels for 57%

profile of v3, /device:TPU:0, one launch (start us, length us, event | category | flops | bytes accessed | tf_op | source)
XLA Modules:
  0.0 170.8 jit_solution(3012302701026458101)
XLA Ops:
  0.7 2.7 %open.1 = (bf16[2,64,2048]{2,1,0:T(8,128)(2,1)}, s32[1]{0:T(128)}) custom-call(s32[4]{0:T(128)} %lengths.3, bf16[4,4,2,64,2048]{4,3,2,1,0:T(8,128)(2,1)} %bitcast.19, bf16[4,4,2,64,2048]{4,3,2,1,0:T(8,128)(2,1)} %bitcast.25), custom_call_target="tpu_custom_call" | custom-call | flops 1000000000 | bytes 1048576 | tf_op jit(solution)/shard_map/open/pallas_call | solution.py:306
  4.0 154.2 %conditional.1 = (bf16[1,1024]{1,0:T(2,128)(2,1)S(1)}, bf16[1,128]{1,0:T(2,128)(2,1)S(1)}, bf16[1,128]{1,0:T(2,128)(2,1)}, f32[1,2048]{1,0:T(1,128)}, bf16[1,204...) conditional(s32[]{:T(128)} %bitcast.6, (s32[4]{0:T(128)S(1)}, ...), branch_computations={%region_0.0_spmd, %region_1.0_spmd, %region_2.0_spmd, %region_3.0_... | conditional | flops 37000003584 | bytes 315784032 | solution.py:577
  4.0 5.6 %branch_0_fun.9 = (bf16[34,2,64,128]{3,2,1,0:T(8,128)(2,1)}, bf16[1,2,2,64,2048]{4,3,2,1,0:T(8,128)(2,1)}) custom-call(s32[4]{0:T(128)S(1)} %get-tuple-element.104.lengths.refs_0_, bf16[4,4,2,64,2048]{4,3,2,1,0:T(8,128)(2,1)} %get-tuple-element.118.k_ref.refs_6_, bf16[4,4,2,64,2048]{4,3,2,1,0:T(8,128)(2,1)} %get-tuple-element.119.v_ref.refs_7_), custom_call_target="tpu_custom_call" | custom-call | flops 1000000000 | bytes 6291456 | tf_op jit(solution)/shard_map/cond/branch_0_fun/pallas_call | solution.py:120
  9.7 2.9 %collective-permute-start = (bf16[34,2,64,128]{3,2,1,0:T(8,128)(2,1)}, bf16[34,2,64,128]{3,2,1,0:T(8,128)(2,1)}, u32[]{:S(2)}, u32[]{:S(2)}) collective-permute-start(bf16[34,2,64,128]{3,2,1,0:T(8,128)(2,1)} %get-tuple-element.121), channel_id=1, source_target_pairs={{0,2},{2,0},{1,3},{3,1},{4,6},{6,4},{5,7},{7,5}} | collective-permute-start | bytes 3342344 | tf_op jit(solution)/shard_map/cond/branch_0_fun/ppermute | solution.py:540
  12.5 5.1 %branch_0_fun.11 = (bf16[34,2,64,128]{3,2,1,0:T(8,128)(2,1)}, bf16[1,2,2,64,2048]{4,3,2,1,0:T(8,128)(2,1)}) custom-call(s32[4]{0:T(128)S(1)} %get-tuple-element.104.lengths.refs_0_, bf16[4,4,2,64,2048]{4,3,2,1,0:T(8,128)(2,1)} %get-tuple-element.118.k_ref.refs_6_, bf16[4,4,2,64,2048]{4,3,2,1,0:T(8,128)(2,1)} %get-tuple-element.119.v_ref.refs_7_), custom_call_target="tpu_custom_call" | custom-call | flops 1000000000 | bytes 6291456 | tf_op jit(solution)/shard_map/cond/branch_0_fun/pallas_call | solution.py:120
  17.7 6.7 %branch_0_fun.13 = (bf16[34,2,64,128]{3,2,1,0:T(8,128)(2,1)}, bf16[2,2,2,64,2048]{4,3,2,1,0:T(8,128)(2,1)}) custom-call(s32[4]{0:T(128)S(1)} %get-tuple-element.104.lengths.refs_0_, bf16[4,4,2,64,2048]{4,3,2,1,0:T(8,128)(2,1)} %get-tuple-element.118.k_ref.refs_6_, bf16[4,4,2,64,2048]{4,3,2,1,0:T(8,128)(2,1)} %get-tuple-element.119.v_ref.refs_7_), custom_call_target="tpu_custom_call" | custom-call | flops 1000000000 | bytes 6291456 | tf_op jit(solution)/shard_map/cond/branch_0_fun/pallas_call | solution.py:120
  24.4 2.0 %collective-permute-start.4 = (bf16[34,2,64,128]{3,2,1,0:T(8,128)(2,1)}, bf16[34,2,64,128]{3,2,1,0:T(8,128)(2,1)S(1)}, u32[]{:S(2)}, u32[]{:S(2)}) collective-permute-start(bf16[34,2,64,128]{3,2,1,0:T(8,128)(2,1)} %get-tuple-element.136), channel_id=1, source_target_pairs={{0,2},{2,0},{1,3},{3,1},{4,6},{6,4},{5,7},{7,5}} | collective-permute-start | bytes 3342344 | tf_op jit(solution)/shard_map/cond/branch_0_fun/ppermute | solution.py:540
  26.4 11.9 %collective-permute-done.refs_9_ = bf16[34,2,64,128]{3,2,1,0:T(8,128)(2,1)} collective-permute-done((bf16[34,2,64,128]{3,2,1,0:T(8,128)(2,1)}, bf16[34,2,64,128]{3,2,1,0:T(8,128)(2,1)}, u32[]{:S(2)}, u32[]{:S(2)}) %collective-permute-start) | collective-permute-done | bytes 1114144 | tf_op jit(solution)/shard_map/cond/branch_0_fun/ppermute | solution.py:540
  38.3 2.0 %collective-permute-start.6 = (bf16[2,64,2048]{2,1,0:T(8,128)(2,1)}, bf16[2,64,2048]{2,1,0:T(8,128)(2,1)}, u32[]{:S(2)}, u32[]{:S(2)}) collective-permute-start(bf16[2,64,2048]{2,1,0:T(8,128)(2,1)} %get-tuple-element.142), channel_id=1, source_target_pairs={{0,2},{2,0},{1,3},{3,1},{4,6},{6,4},{5,7},{7,5}} | collective-permute-start | bytes 1572872 | tf_op jit(solution)/shard_map/cond/branch_0_fun/ppermute | solution.py:536
  40.3 2.6 %payload.4 = (bf16[2,64,2048]{2,1,0:T(8,128)(2,1)}, bf16[2,64,2048]{2,1,0:T(8,128)(2,1)}, bf16[2,64,2048]{2,1,0:T(8,128)(2,1)}) custom-call(bf16[4,4,2,64,2048]{4,3,2,1,0:T(8,128)(2,1)} %get-tuple-element.118.k_ref.refs_6_, bf16[4,4,2,64,2048]{4,3,2,1,0:T(8,128)(2,1)} %get-tuple-element.119.v_ref.refs_7_), custom_call_target="tpu_custom_call" | custom-call | flops 1000000000 | bytes 3145728 | tf_op jit(solution)/shard_map/cond/branch_0_fun/payload/pallas_call | solution.py:148
  42.9 0.6 dynamic_slice.8
  44.2 0.1 pad_maximum_fusion
  44.3 0.1 tile.25.refs_1_.refs_13_
  44.4 0.1 pad_maximum_fusion.1
  44.5 0.1 tile.27.refs_2_.refs_14_
  44.6 17.5 %collective-permute-done.2.refs_9_ = bf16[34,2,64,128]{3,2,1,0:T(8,128)(2,1)} collective-permute-done((bf16[34,2,64,128]{3,2,1,0:T(8,128)(2,1)}, bf16[34,2,64,128]{3,2,1,0:T(8,128)(2,1)}, u32[]{:S(2)}, u32[]{:S(2)}) %collective-permute-start.2) | collective-permute-done | bytes 1114144 | tf_op jit(solution)/shard_map/cond/branch_0_fun/ppermute | solution.py:540
  62.1 16.2 %front.4 = (bf16[1,1024]{1,0:T(2,128)(2,1)S(1)}, bf16[1,128]{1,0:T(2,128)(2,1)S(1)}, bf16[1,128]{1,0:T(2,128)(2,1)S(1)}, f32[1,2048]{1,0:T(1,128)S(1)}, bf16[1,2048]{1,0:T(2,128)(2,1)S(1)}) custom-call(bf16[1,2048]{1,0:T(2,128)(2,1)S(1)} %get-tuple-element.105.h_ref, bf16[4,2048]{1,0:T(4,128)(2,1)S(1)} %get-tuple-element.106.refs_0_.refs_12_, ...), custom_call_target="tpu_custom_call" | custom-call | flops 6000000000 | bytes 40000000 | tf_op jit(solution)/shard_map/cond/branch_0_fun/front/pallas_call | solution.py:266
  78.3 7.5 %collective-permute-done.4.refs_9_ = bf16[34,2,64,128]{3,2,1,0:T(8,128)(2,1)S(1)} collective-permute-done((bf16[34,2,64,128]{3,2,1,0:T(8,128)(2,1)}, bf16[34,2,64,128]{3,2,1,0:T(8,128)(2,1)S(1)}, u32[]{:S(2)}, u32[]{:S(2)}) %collective-permute-start.4) | collective-permute-done | bytes 1114144 | tf_op jit(solution)/shard_map/cond/branch_0_fun/ppermute | solution.py:540
  85.9 0.1 collective-permute-start.8
  86.0 2.1 %collective-permute-start.5 = (bf16[34,2,64,128]{3,2,1,0:T(8,128)(2,1)S(1)}, bf16[34,2,64,128]{3,2,1,0:T(8,128)(2,1)S(1)}, u32[]{:S(2)}, u32[]{:S(2)}) collective-permute-start(bf16[34,2,64,128]{3,2,1,0:T(8,128)(2,1)S(1)} %collective-permute-done.4.refs_9_), channel_id=1, source_target_pairs={{0,1},{1,0},{2,3},{3,2},{4,5},{5,4},{6,7},{7,6}} | collective-permute-start | bytes 3342344 | tf_op jit(solution)/shard_map/cond/branch_0_fun/ppermute | solution.py:541
  88.0 20.1 %branch_0_fun.10 = (bf16[1,1024]{1,0:T(2,128)(2,1)S(1)}, bf16[1,128]{1,0:T(2,128)(2,1)S(1)}, bf16[1,128]{1,0:T(2,128)(2,1)S(1)}, f32[1,2048]{1,0:T(1,128)S(1)}, ...) custom-call(s32[4]{0:T(128)S(1)} %get-tuple-element.104.lengths.refs_0_, ...), custom_call_target="tpu_custom_call" | custom-call | flops 8000000000 | bytes 54525952 | tf_op jit(solution)/shard_map/cond/branch_0_fun/pallas_call | solution.py:439
  108.1 2.7 %branch_0_fun.15 = (bf16[3,2,64,4096]{3,2,1,0:T(8,128)(2,1)}, bf16[3,2,64,4096]{3,2,1,0:T(8,128)(2,1)}) custom-call(bf16[2,64,4096]{2,1,0:T(8,128)(2,1)S(1)} %get-tuple-element.150.wk_ref, bf16[2,64,4096]{2,1,0:T(8,128)(2,1)} %get-tuple-element.151.wv_ref), custom_call_target="tpu_custom_call" | custom-call | flops 1000000000 | bytes 4194304 | tf_op jit(solution)/shard_map/cond/branch_0_fun/pallas_call | solution.py:469
  110.9 0.9 copy-done.13
  111.9 19.1 %branch_0_fun.12 = (bf16[1,1024]{1,0:T(2,128)(2,1)S(1)}, bf16[1,128]{1,0:T(2,128)(2,1)S(1)}, bf16[1,128]{1,0:T(2,128)(2,1)S(1)}, f32[1,2048]{1,0:T(1,128)S(1)}, ...) custom-call(s32[4]{0:T(128)S(1)} %get-tuple-element.104.lengths.refs_0_, ...), custom_call_target="tpu_custom_call" | custom-call | flops 8000000000 | bytes 54525952 | tf_op jit(solution)/shard_map/cond/branch_0_fun/pallas_call | solution.py:439
  131.0 2.7 %branch_0_fun.16 = (bf16[3,2,64,4096]{3,2,1,0:T(8,128)(2,1)}, bf16[3,2,64,4096]{3,2,1,0:T(8,128)(2,1)}) custom-call(bf16[2,64,4096]{2,1,0:T(8,128)(2,1)S(1)} %get-tuple-element.148.wk_ref, bf16[2,64,4096]{2,1,0:T(8,128)(2,1)} %get-tuple-element.149.wv_ref, ...), custom_call_target="tpu_custom_call", output_to_operand_aliasing={{0}: (2, {}), {1}: (3, {})} | custom-call | flops 1000000000 | bytes 4194304 | tf_op jit(solution)/shard_map/cond/branch_0_fun/pallas_call | solution.py:469
  133.8 1.0 copy-done.12
  134.7 20.1 %branch_0_fun.14 = (bf16[1,1024]{1,0:T(2,128)(2,1)S(1)}, bf16[1,128]{1,0:T(2,128)(2,1)S(1)}, bf16[1,128]{1,0:T(2,128)(2,1)}, f32[1,2048]{1,0:T(1,128)}, bf16[1,2...) custom-call(s32[4]{0:T(128)S(1)} %get-tuple-element.104.lengths.refs_0_, ...), custom_call_target="tpu_custom_call" | custom-call | flops 8000000000 | bytes 54525952 | tf_op jit(solution)/shard_map/cond/branch_0_fun/pallas_call | solution.py:439
  154.8 2.7 %branch_0_fun.17 = (bf16[3,2,64,4096]{3,2,1,0:T(8,128)(2,1)}, bf16[3,2,64,4096]{3,2,1,0:T(8,128)(2,1)}) custom-call(bf16[2,64,4096]{2,1,0:T(8,128)(2,1)S(1)} %get-tuple-element.146.wk_ref, bf16[2,64,4096]{2,1,0:T(8,128)(2,1)} %get-tuple-element.147.wv_ref, ...), custom_call_target="tpu_custom_call", output_to_operand_aliasing={{0}: (2, {}), {1}: (3, {})} | custom-call | flops 1000000000 | bytes 4194304 | tf_op jit(solution)/shard_map/cond/branch_0_fun/pallas_call | solution.py:469
  158.3 0.5 copy-done.16
  158.8 7.7 %global.1 = (f32[1,2048]{1,0:T(1,128)S(1)}, bf16[2,64,8192]{2,1,0:T(8,128)(2,1)}, bf16[2,64,8192]{2,1,0:T(8,128)(2,1)}) custom-call(s32[4]{0:T(128)S(1)} %copy-done.14, bf16[1,1024]{1,0:T(2,128)(2,1)S(1)} %get-tuple-element.345.q_ref, bf16[1,128]{1,0:T(2,128)(2,1)} %copy-done.16, bf16[1,128]{1,0:T(2,128)(2,1)} %get-tuple-element.347.vnew_ref, ...), custom_call_target="tpu_custom_call" | custom-call | flops 3000000000 | bytes 14680064 | tf_op jit(solution)/shard_map/global/pallas_call | solution.py:522
  166.5 3.7 %final.1 = bf16[1,2048]{1,0:T(2,128)(2,1)S(1)} custom-call(bf16[1,2048]{1,0:T(2,128)(2,1)S(1)} %get-tuple-element.344.h_ref, f32[1,2048]{1,0:T(1,128)S(1)} %get-tuple-element.354.part_ref), custom_call_target="tpu_custom_call" | custom-call | tf_op jit(solution)/shard_map/final/pallas_call | solution.py:285
  170.2 0.6 copy.98
  (35 shorter events, 0.3 us)
Async XLA Ops:
  0.6 3.4 %copy-start = (bf16[4,2048,128]{2,1,0:T(8,128)(2,1)S(1)}, bf16[4,2048,128]{2,1,0:T(8,128)(2,1)}, u32[]{:S(2)}) copy-start(bf16[4,2048,128]{2,1,0:T(8,128)(2,1)} %param.22) | copy-start | bytes 6291460
  0.6 3.4 %copy-start.9 = (bf16[4,2048]{1,0:T(4,128)(2,1)S(1)}, bf16[4,2048]{1,0:T(4,128)(2,1)}, u32[]{:S(2)}) copy-start(bf16[4,2048]{1,0:T(4,128)(2,1)} %param.20) | copy-start | bytes 49156
  0.7 3.4 %copy-start.14 = (s32[4]{0:T(128)S(1)}, s32[4]{0:T(128)}, u32[]{:S(2)}) copy-start(s32[4]{0:T(128)} %lengths.3) | copy-start | bytes 52
  0.7 3.4 %copy-start.15 = (bf16[1,2048]{1,0:T(2,128)(2,1)S(1)}, bf16[1,2048]{1,0:T(2,128)(2,1)}, u32[]{:S(2)}) copy-start(bf16[1,2048]{1,0:T(2,128)(2,1)} %param.19) | copy-start | bytes 12292
  9.7 28.6 %collective-permute-start = (bf16[34,2,64,128]{3,2,1,0:T(8,128)(2,1)}, bf16[34,2,64,128]{3,2,1,0:T(8,128)(2,1)}, u32[]{:S(2)}, u32[]{:S(2)}) collective-permute-start(bf16[34,2,64,128]{3,2,1,0:T(8,128)(2,1)} %get-tuple-element.121), channel_id=1, source_target_pairs={{0,2},{2,0},{1,3},{3,1},{4,6},{6,4},{5,7},{7,5}} | collective-permute-start | bytes 3342344 | tf_op jit(solution)/shard_map/cond/branch_0_fun/ppermute | solution.py:540
  17.7 44.5 %collective-permute-start.2 = (bf16[34,2,64,128]{3,2,1,0:T(8,128)(2,1)}, bf16[34,2,64,128]{3,2,1,0:T(8,128)(2,1)}, u32[]{:S(2)}, u32[]{:S(2)}) collective-permute-start(bf16[34,2,64,128]{3,2,1,0:T(8,128)(2,1)} %get-tuple-element.129), channel_id=1, source_target_pairs={{0,2},{2,0},{1,3},{3,1},{4,6},{6,4},{5,7},{7,5}} | collective-permute-start | bytes 3342344 | tf_op jit(solution)/shard_map/cond/branch_0_fun/ppermute | solution.py:540
  24.4 61.5 %collective-permute-start.4 = (bf16[34,2,64,128]{3,2,1,0:T(8,128)(2,1)}, bf16[34,2,64,128]{3,2,1,0:T(8,128)(2,1)S(1)}, u32[]{:S(2)}, u32[]{:S(2)}) collective-permute-start(bf16[34,2,64,128]{3,2,1,0:T(8,128)(2,1)} %get-tuple-element.136), channel_id=1, source_target_pairs={{0,2},{2,0},{1,3},{3,1},{4,6},{6,4},{5,7},{7,5}} | collective-permute-start | bytes 3342344 | tf_op jit(solution)/shard_map/cond/branch_0_fun/ppermute | solution.py:540
  38.2 47.7 %collective-permute-start.1 = (bf16[34,2,64,128]{3,2,1,0:T(8,128)(2,1)}, bf16[34,2,64,128]{3,2,1,0:T(8,128)(2,1)}, u32[]{:S(2)}, u32[]{:S(2)}) collective-permute-start(bf16[34,2,64,128]{3,2,1,0:T(8,128)(2,1)} %collective-permute-done.refs_9_), channel_id=1, source_target_pairs={{0,1},{1,0},{2,3},{3,2},{4,5},{5,4},{6,7},{7,6}} | collective-permute-start | bytes 3342344 | tf_op jit(solution)/shard_map/cond/branch_0_fun/ppermute | solution.py:541
  38.3 119.2 %collective-permute-start.6 = (bf16[2,64,2048]{2,1,0:T(8,128)(2,1)}, bf16[2,64,2048]{2,1,0:T(8,128)(2,1)}, u32[]{:S(2)}, u32[]{:S(2)}) collective-permute-start(bf16[2,64,2048]{2,1,0:T(8,128)(2,1)} %get-tuple-element.142), channel_id=1, source_target_pairs={{0,2},{2,0},{1,3},{3,1},{4,6},{6,4},{5,7},{7,5}} | collective-permute-start | bytes 1572872 | tf_op jit(solution)/shard_map/cond/branch_0_fun/ppermute | solution.py:536
  42.9 114.7 %collective-permute-start.7 = (bf16[2,64,2048]{2,1,0:T(8,128)(2,1)}, bf16[2,64,2048]{2,1,0:T(8,128)(2,1)}, u32[]{:S(2)}, u32[]{:S(2)}) collective-permute-start(bf16[2,64,2048]{2,1,0:T(8,128)(2,1)} %get-tuple-element.143), channel_id=1, source_target_pairs={{0,2},{2,0},{1,3},{3,1},{4,6},{6,4},{5,7},{7,5}} | collective-permute-start | bytes 1572872 | tf_op jit(solution)/shard_map/cond/branch_0_fun/ppermute | solution.py:544
  62.1 48.7 %collective-permute-start.3 = (bf16[34,2,64,128]{3,2,1,0:T(8,128)(2,1)}, bf16[34,2,64,128]{3,2,1,0:T(8,128)(2,1)S(1)}, u32[]{:S(2)}, u32[]{:S(2)}) collective-permute-start(bf16[34,2,64,128]{3,2,1,0:T(8,128)(2,1)} %collective-permute-done.2.refs_9_), channel_id=1, source_target_pairs={{0,1},{1,0},{2,3},{3,2},{4,5},{5,4},{6,7},{7,6}} | collective-permute-start | bytes 3342344 | tf_op jit(solution)/shard_map/cond/branch_0_fun/ppermute | solution.py:541
  62.1 25.9 %copy-start.1 = (bf16[4,2048,128]{2,1,0:T(8,128)(2,1)S(1)}, bf16[4,2048,128]{2,1,0:T(8,128)(2,1)}, u32[]{:S(2)}) copy-start(bf16[4,2048,128]{2,1,0:T(8,128)(2,1)} %get-tuple-element.109.refs_5_.refs_17_) | copy-start | bytes 6291460 | tf_op jit(solution)/shard_map/cond
  85.9 22.2 %copy-start.11 = (bf16[34,2,64,128]{3,2,1,0:T(8,128)(2,1)}, bf16[34,2,64,128]{3,2,1,0:T(8,128)(2,1)S(1)}, u32[]{:S(2)}) copy-start(bf16[34,2,64,128]{3,2,1,0:T(8,128)(2,1)S(1)} %collective-permute-done.4.refs_9_) | copy-start | bytes 3342340 | tf_op jit(solution)/shard_map/cond
  85.9 71.6 %collective-permute-start.8 = (bf16[2,64,2048]{2,1,0:T(8,128)(2,1)}, bf16[2,64,2048]{2,1,0:T(8,128)(2,1)}, u32[]{:S(2)}, u32[]{:S(2)}) collective-permute-start(bf16[2,64,2048]{2,1,0:T(8,128)(2,1)} %get-tuple-element.144), channel_id=1, source_target_pairs={{0,3},{3,0},{1,2},{2,1},{4,7},{7,4},{5,6},{6,5}} | collective-permute-start | bytes 1572872 | tf_op jit(solution)/shard_map/cond/branch_0_fun/ppermute | solution.py:545
  86.0 47.8 %collective-permute-start.5 = (bf16[34,2,64,128]{3,2,1,0:T(8,128)(2,1)S(1)}, bf16[34,2,64,128]{3,2,1,0:T(8,128)(2,1)S(1)}, u32[]{:S(2)}, u32[]{:S(2)}) collective-permute-start(bf16[34,2,64,128]{3,2,1,0:T(8,128)(2,1)S(1)} %collective-permute-done.4.refs_9_), channel_id=1, source_target_pairs={{0,1},{1,0},{2,3},{3,2},{4,5},{5,4},{6,7},{7,6}} | collective-permute-start | bytes 3342344 | tf_op jit(solution)/shard_map/cond/branch_0_fun/ppermute | solution.py:541
  108.1 2.8 %copy-start.17 = (bf16[2,64,2048]{2,1,0:T(8,128)(2,1)S(1)}, bf16[2,64,2048]{2,1,0:T(8,128)(2,1)}, u32[]{:S(2)}) copy-start(bf16[2,64,2048]{2,1,0:T(8,128)(2,1)} %get-tuple-element.145) | copy-start | bytes 1572868 | tf_op jit(solution)/shard_map/cond
  110.9 1.0 copy-start.13
  110.9 46.7 %collective-permute-start.9 = (bf16[2,64,2048]{2,1,0:T(8,128)(2,1)S(1)}, bf16[2,64,2048]{2,1,0:T(8,128)(2,1)}, u32[]{:S(2)}, u32[]{:S(2)}) collective-permute-start(bf16[2,64,2048]{2,1,0:T(8,128)(2,1)S(1)} %copy-done.17), channel_id=1, source_target_pairs={{0,3},{3,0},{1,2},{2,1},{4,7},{7,4},{5,6},{6,5}} | collective-permute-start | bytes 1572872 | tf_op jit(solution)/shard_map/cond/branch_0_fun/ppermute | solution.py:546
  131.0 3.8 %copy-start.5 = (bf16[2,2,2,64,2048]{4,3,2,1,0:T(8,128)(2,1)S(1)}, bf16[2,2,2,64,2048]{4,3,2,1,0:T(8,128)(2,1)}, u32[]{:S(2)}) copy-start(bf16[2,2,2,64,2048]{4,3,2,1,0:T(8,128)(2,1)} %get-tuple-element.372.refs_8_) | copy-start | bytes 6291460 | tf_op jit(solution)/shard_map/cond
  133.7 1.0 copy-start.12
  158.3 0.5 copy-start.16
